TPU v7x, 32 devices: a whole 2x2x4 slice. The times are simulated.
32 devices in a mesh: section: 2 (over y), ep: 16 (over z, x, core).
Axes of the slice: x: 2, y: 2, z: 4, core: 2. Of those that a mesh axis runs over, the one named last changes fastest.
Arguments:
- inputs: bfloat16 [2, 2048, 1536], P('section', 'ep'), may hold values from -6 to 6
- upstream: bfloat16 [2, 2048, 1536], P('section', 'ep'), may hold values from -6 to 6
- gate_saved: bfloat16 [2, 2048, 8, 384], P('section', 'ep'), may hold values from -6 to 6
- expert_ids: int32 [2, 2048, 8], P('section', 'ep'), may hold values from 0 to 31, all different within a row; in each aligned block of 128 rows (0 to 127, 128 to 255, ..., all dimensions but the last counted through in order) at most 48 rows name the same one
- route_weights: float32 [2, 2048, 8], P('section', 'ep'), may hold values from 0.05 to 0.5
- w_up: bfloat16 [2, 32, 1536, 384], P('section', 'ep'), may hold values from -0.15625 to 0.15625
- w_down: bfloat16 [2, 32, 384, 1536], P('section', 'ep'), may hold values from -0.3125 to 0.3125
Outputs:
- delivered: bfloat16 [2, 2048, 1536], P('section', 'ep')
- grad_up: bfloat16 [2, 32, 1536, 384], P('section', 'ep')
- grad_down: bfloat16 [2, 32, 384, 1536], P('section', 'ep')
Inputs may be any that keep to these rules, and one draw needn't show every extreme that they name: `expert_ids`: each row names 8 different experts. In the rows of one device no expert is named more than 48 times, and in every draw some expert is named exactly 48 times in the rows of some device; every expert is named somewhere.
All inputs are finite; a program needn't handle non-finite values.
Results may differ from a plain program's by a relative error of at most 0.012.
Values may be sent and summed in bfloat16 or wider, within the bound.
A program may use at most 192 MiB of HBM per device.

v0:
```python
import jax
import jax.numpy as jnp
from jax import lax
from jax.sharding import PartitionSpec as P

BF16 = jnp.bfloat16
F32 = jnp.float32


def from_behind(block, axis, distance):
    devices = range(lax.axis_size(axis))
    route = [((i - distance) % len(devices), i) for i in devices]
    return lax.ppermute(block, axis, route)


def body(inputs, upstream, gate_saved, expert_ids, route_weights, w_up, w_down):
    ep = lax.axis_size("ep")
    local = w_up.shape[1]
    experts = local * ep
    toks, top = expert_ids.shape[1:]
    cap = 3 * toks * top // (2 * experts)
    width = inputs.shape[2]
    ff = w_up.shape[3]

    routing = jnp.concatenate([expert_ids[0].astype(F32), route_weights[0]], axis=1)
    routing_all = lax.all_gather(routing, "ep", axis=0, tiled=False)

    ids = expert_ids[0]
    hit = ids[:, :, None] == jnp.arange(experts, dtype=jnp.int32)
    member = jnp.any(hit, axis=1).astype(BF16)
    lower = (jnp.arange(toks)[:, None] > jnp.arange(toks)[None, :]).astype(BF16)
    rank = jnp.dot(lower, member, preferred_element_type=F32)
    place = jnp.sum(jnp.where(hit, rank[:, None, :], 0.0), axis=2)
    slot = (ids * cap + place.astype(jnp.int32)).reshape(1, toks * top)
    pick = (jnp.arange(experts * cap, dtype=jnp.int32)[:, None] == slot).astype(BF16)
    gate_send = jnp.dot(pick, gate_saved[0].reshape(toks * top, ff), preferred_element_type=F32)
    gate_send = gate_send.astype(BF16).reshape(ep, local, cap, ff)
    gate_recv = lax.all_to_all(gate_send, "ep", split_axis=0, concat_axis=0, tiled=True)

    cot = from_behind(upstream, "section", -1)[0]
    x_all = lax.all_gather(inputs[0], "ep", axis=0, tiled=True)
    c_all = lax.all_gather(cot, "ep", axis=0, tiled=True)

    me = lax.axis_index("ep")
    mine = (me * local + jnp.arange(local)).astype(F32)
    hits = routing_all[:, :, :top, None] == mine
    weight = jnp.sum(jnp.where(hits, routing_all[:, :, top:, None], 0.0), axis=2)
    members = jnp.any(hits, axis=2)
    ranks = jnp.einsum("ab,sbe->sae", lower, members.astype(BF16), preferred_element_type=F32)
    ranks = jnp.where(members, ranks, -1.0)
    spread = (ranks[:, :, :, None] == jnp.arange(cap).astype(F32)).astype(BF16)
    gate = jnp.einsum("stec,secf->stef", spread, gate_recv, preferred_element_type=F32)
    act = jax.nn.silu(gate).reshape(ep * toks, local, ff)
    weight = weight.reshape(ep * toks, local, 1)
    act_w = (act * weight)

    up = w_up[0]
    down = w_down[0]
    up_cat = jnp.transpose(up, (1, 0, 2)).reshape(width, local * ff)
    down_cat = down.reshape(local * ff, width)
    act_w = act_w.reshape(ep * toks, local * ff)
    u = jnp.dot(x_all, up_cat, preferred_element_type=F32)
    hidden = (act_w * u).astype(BF16)
    h = lax.dot_general(c_all, down_cat, (((1,), (1,)), ((), ())), preferred_element_type=F32)
    g = (act_w * h).astype(BF16)
    part = lax.dot_general(g, up_cat, (((1,), (1,)), ((), ())), preferred_element_type=F32)
    grad = lax.psum_scatter(part.astype(BF16), "ep", scatter_dimension=0, tiled=True)
    delivered = from_behind(grad[None], "section", -1)
    grad_down = lax.dot_general(hidden, c_all, (((0,), (0,)), ((), ())), preferred_element_type=F32)
    grad_up = jnp.stack([
        lax.dot_general(x_all, g[:, e * ff:(e + 1) * ff], (((0,), (0,)), ((), ())), preferred_element_type=F32)
        for e in range(local)
    ])
    return (
        delivered,
        grad_up.astype(BF16)[None],
        grad_down.astype(BF16).reshape(1, local, ff, width),
    )


def solution(mesh):
    return jax.shard_map(
        body,
        mesh=mesh,
        in_specs=(
            P("section", "ep", None),
            P("section", "ep", None),
            P("section", "ep", None, None),
            P("section", "ep", None),
            P("section", "ep", None),
            P("section", "ep", None, None),
            P("section", "ep", None, None),
        ),
        out_specs=(
            P("section", "ep", None),
            P("section", "ep", None, None),
            P("section", "ep", None, None),
        ),
        check_vma=False,
    )
```

profile of v0, /device:TPU:0, one launch (start us, length us, event | category | flops | bytes accessed | tf_op | source)
XLA Modules:
  0.0 272.7 jit_solution(5686237098454286970)
XLA Ops:
  7.2 0.0 copy-start
  7.2 0.0 all-gather.6.cloned.1.call-start
  7.2 3.1 %collective-permute-start = (bf16[1,128,1536]{2,1,0:T(8,128)(2,1)}, bf16[1,128,1536]{2,1,0:T(8,128)(2,1)S(1)}, u32[]{:S(2)}, u32[]{:S(2)}) collective-permute-start(bf16[1,128,1536]{2,1,0:T(8,128)(2,1)} %param.8), channel_id=1, source_target_pairs={{16,0},{0,16},{17,1},{1,17},{18,2},{2,18},{19,3},{3,19},{20,4},{4,... | collective-permute-start | bytes 1179656 | tf_op jit(solution)/shard_map/ppermute | solution.py:13
  10.3 9.3 %collective-permute-done = bf16[1,128,1536]{2,1,0:T(8,128)(2,1)S(1)} collective-permute-done((bf16[1,128,1536]{2,1,0:T(8,128)(2,1)}, bf16[1,128,1536]{2,1,0:T(8,128)(2,1)S(1)}, u32[]{:S(2)}, u32[]{:S(2)}) %collective-permute-start) | collective-permute-done | bytes 393248 | tf_op jit(solution)/shard_map/ppermute | solution.py:13
  19.6 0.0 copy-start.4
  19.6 0.7 copy-done.4
  20.4 0.0 all-gather.6.cloned.1.call-update
  20.4 0.0 all-gather.8.cloned.1.call-start
  20.4 0.7 all-gather.8.cloned.1.call-update
  21.1 0.7 bitcast_convert_fusion
  21.8 0.1 copy.35
  21.9 0.1 mul.41
  22.0 0.7 fusion.45
  22.7 0.1 fusion.47
  22.9 0.7 select_reduce_fusion
  23.6 0.1 copy.36
  23.7 0.1 convert_element_type.56
  23.8 0.0 copy-start.5
  23.8 4.0 %fusion.22 = bf16[1536,384]{1,0:T(8,128)(2,1)} fusion(s32[1024]{0:T(1024)S(1)} %add.23, bf16[1,128,8,384]{3,2,1,0:T(8,128)(2,1)} %param.9), kind=kOutput, calls=%fused_computation.22 | convolution fusion | flops 1210122240 | bytes 1970176 | tf_op jit(solution)/shard_map/dot_general | solution.py:36
  27.8 6.2 %all-to-all-start = ((bf16[16,2,48,384]{3,2,1,0:T(8,128)(2,1)}), bf16[16,2,48,384]{3,2,1,0:T(8,128)(2,1)}, u32[]{:S(2)}, u32[]{:S(2)}) async-start(bf16[16,2,48,384]{3,2,1,0:T(8,128)(2,1)} %bitcast.2), calls=%async_computation | async-start | bytes 2359296 | tf_op jit(solution)/shard_map/all_to_all | solution.py:38
  34.0 0.0 reduce-scatter.2.cloned.1.call-start
  34.0 0.0 copy-done.5
  34.0 45.0 %all-gather = f32[2048,16]{0,1:T(8,128)S(1)} all-gather(f32[128,16]{0,1:T(8,128)S(1)} %pad_maximum_fusion.1), channel_id=2, replica_groups=mesh['section'=2,'ep'=16] {'ep'}, dimensions={0}, use_global_device_ids=true | all-gather | bytes 139264 | tf_op jit(solution)/shard_map/all_gather | solution.py:26
  79.1 0.1 compare_reduce_fusion
  79.2 0.1 fusion.37
  79.4 0.1 fusion.44
  79.6 0.4 copy.43
  79.9 4.8 %mul.45 = f32[2048,2,384]{2,1,0:T(2,128)S(1)} broadcast(f32[2048,2]{1,0:T(8,128)S(1)} %copy.43), dimensions={0,1} | broadcast | bytes 6307840 | tf_op jit(solution)/shard_map/mul | solution.py:55
  84.8 3.0 %copy.53 = f32[256,8,2,384]{3,1,2,0:T(8,128)} copy(f32[256,8,2,384]{3,2,1,0:T(2,128)S(1)} %bitcast.86) | data formatting | bytes 12582912
  87.8 4.3 %copy.45 = bf16[1,2,1536,384]{2,3,1,0:T(8,128)(2,1)} copy(bf16[1,2,1536,384]{3,2,1,0:T(8,128)(2,1)} %param.12) | data formatting | bytes 4718592 | tf_op args[5]
  92.1 0.0 all-to-all-done
  92.1 5.8 %bitcast_multiply_fusion = f32[16,128,2,384]{1,3,2,0:T(8,128)} fusion(bf16[16,2,48,384]{3,2,1,0:T(8,128)(2,1)} %all-to-all-done, f32[16,128,2]{1,2,0:T(2,128)S(1)} %copy.40, f32[48]{0:T(128)S(1)} %iota_convert_fusion), kind=kOutput, calls=%fused_computation.11 | convolution fusion | flops 157483008 | bytes 7487680 | tf_op jit(solution)/shard_map/stec,secf->stef/dot_general | solution.py:52
  97.8 10.3 %copy.47 = f32[16,128,2,384]{3,2,1,0:T(2,128)} copy(f32[16,128,2,384]{1,3,2,0:T(8,128)} %bitcast_multiply_fusion) | data formatting | bytes 12582912 | tf_op jit(solution)/shard_map/reshape | solution.py:53
  108.2 6.1 %copy.52 = f32[256,8,2,384]{3,1,2,0:T(8,128)} copy(f32[256,8,2,384]{3,2,1,0:T(2,128)} %bitcast.87) | data formatting | bytes 12582912
  114.2 0.0 all-gather.6.cloned.1.call-done
  114.2 0.0 copy-done
  114.2 0.0 copy-start.2
  114.2 10.2 %multiply_convert_fusion.1 = bf16[2048,768]{1,0:T(8,128)(2,1)S(1)} fusion(bf16[768,1536]{1,0:T(8,128)(2,1)S(1)} %bitcast.85, bf16[1,2048,1536]{2,1,0:T(8,128)(2,1)} %all-gather.6.cloned.1.call-done, f32[2048,768]{1,0:T(8,128)} %bitcast.90, f32[2048,768]{1,0:T(8,128)} %bitcast.88), kind=kOutput, calls=%fused_computation.17 | convolution fusion | flops 4836556800 | bytes 24379392 | tf_op jit(solution)/shard_map/dot_general | solution.py:64
  124.5 0.0 copy-start.6
  124.5 1.6 copy-done.6
  126.1 0.0 copy-done.2
  126.1 6.9 %convolution_convert_fusion = bf16[2048,1536]{1,0:T(8,128)(2,1)} fusion(bf16[2048,768]{1,0:T(8,128)(2,1)S(1)} %multiply_convert_fusion.1, bf16[1536,768]{0,1:T(8,128)(2,1)S(1)} %bitcast.92), kind=kOutput, calls=%fused_computation | convolution fusion | flops 4834983936 | bytes 11796480 | tf_op jit(solution)/shard_map/dot_general | solution.py:66
  133.0 0.0 reduce-scatter.2.cloned.1.call-update
  133.1 0.0 copy-start.3
  133.1 30.3 %all-gather.8.cloned.1.call-done = bf16[1,2048,1536]{2,1,0:T(8,128)(2,1)} async-done(((bf16[1,128,1536]{2,1,0:T(8,128)(2,1)}), bf16[1,2048,1536]{2,1,0:T(8,128)(2,1)}) %all-gather.8.cloned.1.call-update) | async-done | bytes 6291472 | tf_op jit(solution)/shard_map/all_gather | solution.py:41
  163.4 5.9 %fusion.29 = bf16[1,1,1536,384]{2,3,1,0:T(8,128)(2,1)S(1)} fusion(bf16[1,2048,1536]{2,1,0:T(8,128)(2,1)} %all-gather.8.cloned.1.call-done, bf16[2048,768]{1,0:T(8,128)(2,1)} %copy-done.6), kind=kOutput, calls=%fused_computation.25 | convolution fusion | flops 2416508928 | bytes 9043968 | tf_op jit(solution)/shard_map/dot_general | solution.py:71
  169.3 0.0 copy-done.3
  169.3 30.7 %fusion.18 = bf16[768,1536]{1,0:T(8,128)(2,1)} fusion(bf16[1,2048,1536]{2,1,0:T(8,128)(2,1)} %all-gather.6.cloned.1.call-done, bf16[1536,768]{0,1:T(8,128)(2,1)S(1)} %bitcast.93, bf16[1,2048,1536]{2,1,0:T(8,128)(2,1)} %all-gather.8.cloned.1.call-done, f32[2048,768]{1,0:T(8,128)} %bitcast.91, f32[2048,768]{1,0:T(8,128)} %bitcast.89), kind=kOutput, calls=%fused_computation.20 | convolution fusion | flops 9669574656 | bytes 29884416 | tf_op jit(solution)/shard_map/dot_general | solution.py:69
  200.0 51.1 %reduce-scatter.2.cloned.1.call-done = bf16[128,1536]{1,0:T(8,128)(2,1)} async-done(((bf16[2048,1536]{1,0:T(8,128)(2,1)}), bf16[128,1536]{1,0:T(8,128)(2,1)}) %reduce-scatter.2.cloned.1.call-update) | async-done | bytes 393232 | tf_op jit(solution)/shard_map/reduce_scatter | solution.py:67
  251.1 1.5 collective-permute-start.1
  252.6 5.9 %fusion.32 = bf16[1,1,1536,384]{2,3,1,0:T(8,128)(2,1)S(1)} fusion(bf16[1,2048,1536]{2,1,0:T(8,128)(2,1)} %all-gather.8.cloned.1.call-done, bf16[2048,768]{1,0:T(8,128)(2,1)} %copy-done.6), kind=kOutput, calls=%fused_computation.26 | convolution fusion | flops 2416508928 | bytes 9043968 | tf_op jit(solution)/shard_map/dot_general | solution.py:71
  258.5 0.0 copy-start.1
  258.5 1.6 pad_maximum_fusion
  260.2 4.3 %copy.46 = bf16[1,2,1536,384]{3,2,1,0:T(8,128)(2,1)} copy(bf16[1,2,1536,384]{2,3,1,0:T(8,128)(2,1)} %pad_maximum_fusion) | data formatting | bytes 4718592
  264.4 0.0 collective-permute-done.1
  264.4 1.8 copy.57
  266.2 0.0 copy-done.1
  (10 shorter events, 0.1 us)
Async XLA Ops:
  7.2 107.1 %copy-start = (bf16[1,2,384,1536]{3,2,1,0:T(8,128)(2,1)S(1)}, bf16[1,2,384,1536]{3,2,1,0:T(8,128)(2,1)}, u32[]{:S(2)}) copy-start(bf16[1,2,384,1536]{3,2,1,0:T(8,128)(2,1)} %param.13) | copy-start | bytes 7077892
  7.2 107.1 %all-gather.6.cloned.1.call-start = ((), (), s32[]{:S(2)}) async-start(), calls=%async_computation.3 | async-start | bytes 6684672 | tf_op jit(solution)/shard_map/all_gather | solution.py:42
  7.2 12.4 %collective-permute-start = (bf16[1,128,1536]{2,1,0:T(8,128)(2,1)}, bf16[1,128,1536]{2,1,0:T(8,128)(2,1)S(1)}, u32[]{:S(2)}, u32[]{:S(2)}) collective-permute-start(bf16[1,128,1536]{2,1,0:T(8,128)(2,1)} %param.8), channel_id=1, source_target_pairs={{16,0},{0,16},{17,1},{1,17},{18,2},{2,18},{19,3},{3,19},{20,4},{4,... | collective-permute-start | bytes 1179656 | tf_op jit(solution)/shard_map/ppermute | solution.py:13
  19.6 0.7 copy-start.4
  20.4 143.0 %all-gather.8.cloned.1.call-start = ((), (), s32[]{:S(2)}) async-start(), calls=%async_computation.4 | async-start | bytes 6684672 | tf_op jit(solution)/shard_map/all_gather | solution.py:41
  23.8 10.2 %copy-start.5 = (f32[1,128,8]{1,2,0:T(8,128)S(1)}, f32[1,128,8]{1,2,0:T(8,128)}, u32[]{:S(2)}) copy-start(f32[1,128,8]{1,2,0:T(8,128)} %param.11) | copy-start | bytes 12292
  27.8 64.3 %all-to-all-start = ((bf16[16,2,48,384]{3,2,1,0:T(8,128)(2,1)}), bf16[16,2,48,384]{3,2,1,0:T(8,128)(2,1)}, u32[]{:S(2)}, u32[]{:S(2)}) async-start(bf16[16,2,48,384]{3,2,1,0:T(8,128)(2,1)} %bitcast.2), calls=%async_computation | async-start | bytes 2359296 | tf_op jit(solution)/shard_map/all_to_all | solution.py:38
  34.0 217.2 %reduce-scatter.2.cloned.1.call-start = ((), (), s32[]{:S(2)}) async-start(), calls=%async_computation.2 | async-start | bytes 6684672 | tf_op jit(solution)/shard_map/reduce_scatter | solution.py:67
  114.2 11.9 %copy-start.2 = (bf16[1,2,1536,384]{2,3,1,0:T(8,128)(2,1)S(1)}, bf16[1,2,1536,384]{2,3,1,0:T(8,128)(2,1)}, u32[]{:S(2)}) copy-start(bf16[1,2,1536,384]{2,3,1,0:T(8,128)(2,1)} %copy.45) | copy-start | bytes 7077892
  124.5 1.6 copy-start.6
  133.1 36.2 %copy-start.3 = (bf16[1,2,1536,384]{2,3,1,0:T(8,128)(2,1)S(1)}, bf16[1,2,1536,384]{2,3,1,0:T(8,128)(2,1)}, u32[]{:S(2)}) copy-start(bf16[1,2,1536,384]{2,3,1,0:T(8,128)(2,1)} %copy.45) | copy-start | bytes 7077892
  251.1 13.3 %collective-permute-start.1 = (bf16[1,128,1536]{2,1,0:T(8,128)(2,1)}, bf16[1,128,1536]{2,1,0:T(8,128)(2,1)}, u32[]{:S(2)}, u32[]{:S(2)}) collective-permute-start(bf16[1,128,1536]{2,1,0:T(8,128)(2,1)} %bitcast.100), channel_id=1, source_target_pairs={{16,0},{0,16},{17,1},{1,17},{18,2},{2,18},{19,3},{3,19},{20,4},{4,... | collective-permute-start | bytes 1179656 | tf_op jit(solution)/shard_map/ppermute | solution.py:13
  258.5 7.7 %copy-start.1 = (bf16[1,2,384,1536]{3,2,1,0:T(8,128)(2,1)S(1)}, bf16[1,2,384,1536]{3,2,1,0:T(8,128)(2,1)}, u32[]{:S(2)}) copy-start(bf16[1,2,384,1536]{3,2,1,0:T(8,128)(2,1)} %param.13) | copy-start | bytes 7077892
Sparse Core Ops, SparseCore 0:
  20.5 80.3 all-gather.5
  103.2 60.1 all-gather.7
  167.3 83.7 reduce-scatter.1
where the time goes:
time: 274 us; the launch traced here: 273 us
  waiting for transfers between devices  91.5 us (33%)
  matrix products  69.7 us (25%)
  blocking collectives  45 us (16%)
  local copies, waits for them, and re-layouts  37.8 us (14%)
  between operations  13.9 us (5%)
  starting transfers between devices  10.8 us (4%)
  other arithmetic  4 us (1%)
    reduce_scatter x1, waiting for transfers between devices, body(): lax.psum_scatter(part.astype(BF16), 'ep', scatter_dimension=0, tiled=True)  51.1 us
    all_gather x1, blocking collectives, body(): routing_all = lax.all_gather(routing, 'ep', axis=0, tiled=False)  45 us
    dot_general x1, matrix products, body(): lax.dot_general(hidden, c_all, (((0,), (0,)), ((), ())), preferred_elemen...  30.7 us
    all_gather x1, waiting for transfers between devices, body(): x_all = lax.all_gather(inputs[0], 'ep', axis=0, tiled=True)  30.3 us
    unnamed x22, local copies, waits for them, and re-layouts  21.9 us
    dot_general x2, matrix products, body(): lax.dot_general(x_all, g[:, e * ff:(e + 1) * ff], (((0,), (0,)), ((), ())...  11.8 us
    reshape x1, local copies, waits for them, and re-layouts, body(): act = jax.nn.silu(gate).reshape(ep * toks, local, ff)  10.3 us
    dot_general x1, matrix products, body(): lax.dot_general(c_all, down_cat, (((1,), (1,)), ((), ())), preferred_elem...  10.2 us
  transfers between devices with their start and end apart: 6, of which 3 were waited for; matrix products, arithmetic and copies ran while one was open for 39% of the time, Pallas kernels for 0%

commit v1 on v0

--- a/solution.py
+++ b/solution.py
@@ -1,10 +1,441 @@
+import functools
+
 import jax
 import jax.numpy as jnp
 from jax import lax
+from jax.experimental import pallas as pl
+from jax.experimental.pallas import tpu as pltpu
 from jax.sharding import PartitionSpec as P
 
 BF16 = jnp.bfloat16
 F32 = jnp.float32
+MESH = pl.DeviceIdType.MESH
+VMEM_BYTES = 67_000_000
+TN = (((0,), (0,)), ((), ()))
+NT = (((1,), (1,)), ((), ()))
+
+
+def dot(a, b, dims=(((1,), (0,)), ((), ()))):
+    return lax.dot_general(a, b, dims, preferred_element_type=F32)
+
+
+def iota(shape, dim):
+    return lax.broadcasted_iota(jnp.int32, shape, dim)
+
+
+def kernel(
+    ns, ep, toks, top, width, ff, local, cap,
+    x_in, up_in, gate_in, wup_in, wdn_in, idr_ref, wr_ref, idt_ref,
+    out_ref, gup_ref, gdn_ref,
+    xc, pay, paysend, idt, gate, act, slots, wup, wdn, dense, hid, grd, part,
+    own, sibsend, sibrecv, rss, rsr, fin, gtile, dtile,
+    ring_s, ring_r, sib_s, sib_r, pay_s, pay_r, id_s, id_r, ps_s, ps_r, rs_s, rs_r,
+    y_s, y_r, loc, gsem, dsem,
+):
+    n = ep // 2
+    half = n // 2
+    sec = lax.axis_index("section")
+    me = lax.axis_index("ep")
+    core = lax.rem(me, 2)
+    chip = lax.div(me, 2)
+    sib = me + 1 - 2 * core
+    a, b = lax.div(chip, 2), lax.rem(chip, 2)
+    pos = (1 - b) * a + b * (n - 1 - a)
+    w2 = width // 2
+    lff = local * ff
+    lcap = local * cap
+    two = 2 * toks
+
+    def chip_at(q):
+        h = lax.div(q, half)
+        return (1 - h) * (2 * q) + h * (2 * (n - 1 - q) + 1)
+
+    def rows(dev):
+        return pl.ds(pl.multiple_of(dev * toks, toks), toks)
+
+    def here(dev):
+        return (sec, dev)
+
+    def remote(src, dst, s, r, to):
+        return pltpu.make_async_remote_copy(
+            src_ref=src, dst_ref=dst, send_sem=s, recv_sem=r, device_id=to, device_id_type=MESH
+        )
+
+    nxt = [chip_at(lax.rem(pos + 1, n)) * 2 + core, chip_at(lax.rem(pos + n - 1, n)) * 2 + core]
+    sec_to = lax.rem(sec + ns - 1, ns)
+    sec_from = lax.rem(sec + 1, ns)
+
+    bar = pltpu.get_barrier_semaphore()
+    greet = [(sec_to, me)] + ([(sec_from, me)] if ns > 2 else [])
+
+    def hello(i, _):
+        pl.semaphore_signal(bar, inc=1, device_id=here(lax.rem(me + i, ep)), device_id_type=MESH)
+        return 0
+
+    for to in greet:
+        pl.semaphore_signal(bar, inc=1, device_id=to, device_id_type=MESH)
+    lax.fori_loop(1, ep, hello, 0)
+
+    local_copies = [
+        pltpu.make_async_copy(x_in, xc.at[0, rows(me)], loc.at[0]),
+        pltpu.make_async_copy(gate_in, gate, loc.at[1]),
+        pltpu.make_async_copy(wdn_in, wdn, loc.at[2]),
+    ] + [
+        pltpu.make_async_copy(wup_in.at[e], wup.at[:, pl.ds(e * ff, ff)], loc.at[3 + e]) for e in range(local)
+    ]
+    for c in local_copies:
+        c.start()
+    pl.semaphore_wait(bar, ep - 1 + len(greet))
+
+    def ridx(d, s, piece):
+        return (d * (half + 1) + s) * 2 + piece
+
+    def ring(src, piece, dev, d, s):
+        i = ridx(d, s, piece)
+        return remote(src, xc.at[piece, rows(dev)], ring_s.at[i], ring_r.at[i], here(nxt[d]))
+
+    def side(src, piece, dev, r):
+        i = r * 2 + piece
+        return remote(src, xc.at[piece, rows(dev)], sib_s.at[i], sib_r.at[i], here(sib))
+
+    cot = remote(up_in, xc.at[1, rows(me)], y_s.at[0], y_r.at[0], (sec_to, me))
+    cot.start()
+    for d in (0, 1):
+        ring(x_in, 0, me, d, 1).start()
+    side(x_in, 0, me, 0).start()
+    idt[me] = idt_ref[...]
+
+    def tell(i, _):
+        to = lax.rem(me + i, ep)
+        remote(idt_ref, idt.at[me], id_s.at[i], id_r.at[me], here(to)).start()
+        return 0
+
+    lax.fori_loop(1, ep, tell, 0)
+
+    experts = ep * local
+    lanes = idr_ref.shape[1]
+    tri = (iota((lanes, lanes), 0) < iota((lanes, lanes), 1)).astype(BF16)
+    base = jnp.zeros((experts, 1), F32)
+    for k in range(idr_ref.shape[0]):
+        ids = idr_ref[k : k + 1, :]
+        hot = (iota((experts, lanes), 0).astype(F32) == ids).astype(F32)
+        cum = dot(hot.astype(BF16), tri) + base
+        base = base + jnp.sum(hot, axis=1, keepdims=True)
+        slots[k : k + 1, :] = ids * cap + jnp.sum(hot * cum, axis=0, keepdims=True)
+
+    local_copies[1].wait()
+
+    def silu_rows(k, _):
+        r = pl.ds(pl.multiple_of(k * lanes, lanes), lanes)
+        v = gate[r, :].astype(F32)
+        act[r, :] = (v / (1.0 + jnp.exp(-v))).astype(BF16)
+        return 0
+
+    lax.fori_loop(0, idr_ref.shape[0], silu_rows, 0)
+    group = 4 * lcap
+
+    def pack(m, _):
+        acc = jnp.zeros((group, ff), F32)
+        at = (iota((group, lanes), 0) + m * group).astype(F32)
+        for k in range(idr_ref.shape[0]):
+            pick = jnp.where(at == slots[k : k + 1, :], wr_ref[k : k + 1, :], 0.0).astype(BF16)
+            acc = acc + dot(pick, act[k * lanes : (k + 1) * lanes, :])
+        for j in range(4):
+            paysend[m * 4 + j] = acc[j * lcap : (j + 1) * lcap].astype(BF16)
+        return 0
+
+    lax.fori_loop(0, ep // 4, pack, 0)
+
+    def give(i, _):
+        to = lax.rem(me + i, ep)
+        remote(paysend.at[to], pay.at[me], pay_s.at[i], pay_r.at[me], here(to)).start()
+        return 0
+
+    lax.fori_loop(1, ep, give, 0)
+    pay[me] = paysend[me]
+
+    cot.wait_recv()
+    for d in (0, 1):
+        ring(xc.at[1, rows(me)], 1, me, d, 1).start()
+    side(xc.at[1, rows(me)], 1, me, 0).start()
+    for c in [local_copies[0]] + local_copies[2:]:
+        c.wait()
+
+    upper = (iota((toks, toks), 0) < iota((toks, toks), 1)).astype(BF16)
+
+    def arrive(piece, dev, d, s):
+        ring(xc.at[piece, rows(dev)], piece, dev, d, s).wait_recv()
+
+    def chunk(r):
+        q = chip_at(lax.rem(pos + r, n))
+        other = q * 2 + 1 - core
+        for piece in (0, 1):
+            side(xc.at[piece, rows(other)], piece, other, r).wait_recv()
+        for j in (0, 1):
+            src = q * 2 + j
+
+            @pl.when(src != me)
+            def _():
+                remote(paysend.at[src], pay.at[src], pay_s.at[0], pay_r.at[src], here(src)).wait_recv()
+                remote(idt_ref, idt.at[src], id_s.at[0], id_r.at[src], here(src)).wait_recv()
+
+            names = idt[src]
+            for e in range(local):
+                mine = (me * local + e).astype(F32)
+                member = jnp.sum((names == mine).astype(F32), axis=0, keepdims=True)
+                rank = dot(jnp.broadcast_to(member, (8, toks)).astype(BF16), upper)[0:1, :]
+                key = jnp.where(member > 0.0, rank, -1.0)
+                spread = (iota((cap, toks), 0).astype(F32) == key).astype(BF16)
+                dense[j * toks : (j + 1) * toks, e * ff : (e + 1) * ff] = dot(
+                    spread, pay[src, e * cap : (e + 1) * cap, :], TN
+                )
+        both = pl.ds(pl.multiple_of(q * two, two), two)
+        u = dot(xc[0, both, :], wup[...])
+        hid[both, :] = (dense[...] * u).astype(BF16)
+        h = dot(xc[1, both, :], wdn[...], NT)
+        g = (dense[...] * h).astype(BF16)
+        grd[both, :] = g
+        part[...] = dot(g, wup[...], NT)
+        sibsend[r] = part[pl.ds(pl.multiple_of((1 - core) * toks, toks), toks), :].astype(BF16)
+        remote(sibsend.at[r], sibrecv.at[r], ps_s.at[r], ps_r.at[r], here(sib)).start()
+        own[r] = part[pl.ds(pl.multiple_of(core * toks, toks), toks), :]
+
+    def event(it, _):
+        s = lax.div(it, 2) + 1
+        piece = lax.rem(it, 2)
+
+        @pl.when(it < 2 * (half - 1))
+        def _():
+            for d in (0, 1):
+                r = (n - s) if d == 0 else s
+                dev = chip_at(lax.rem(pos + r, n)) * 2 + core
+                arrive(piece, dev, d, s)
+                src = xc.at[piece, rows(dev)]
+
+                @pl.when((s + 1 < half) | (piece == d))
+                def _():
+                    ring(src, piece, dev, d, s + 1).start()
+
+                side(src, piece, dev, r).start()
+
+        @pl.when(it == 2 * half)
+        def _():
+            for d in (0, 1):
+                dev = chip_at(lax.rem(pos + half, n)) * 2 + core
+                arrive(d, dev, d, half)
+                side(xc.at[d, rows(dev)], d, dev, half).start()
+
+        @pl.when(it != 1)
+        def _():
+            dist = lax.div(it, 2)
+            chunk((1 - piece) * dist + piece * (n - dist))
+
+        return 0
+
+    lax.fori_loop(0, 2 * half + 1, event, 0)
+
+    cols = [slice(0, w2), slice(w2, width)]
+
+    def xsum(d, t, c):
+        i = (d * (half + 1) + t) * 2 + c
+        return remote(
+            rss.at[d, t - 1, :, cols[c]], rsr.at[d, t - 1, :, cols[c]], rs_s.at[i], rs_r.at[i], here(nxt[d])
+        )
+
+    def sib_part(r):
+        remote(sibsend.at[r], sibrecv.at[r], ps_s.at[r], ps_r.at[r], here(sib)).wait_recv()
+
+    def base_sum(r, c):
+        return own[r, :, cols[c]] + sibrecv[r, :, cols[c]].astype(F32)
+
+    def up_copy(i, slot):
+        return [
+            pltpu.make_async_copy(
+                gtile.at[slot, e], gup_ref.at[e, pl.ds(i * 256, 256), :], gsem.at[slot * local + e]
+            )
+            for e in range(local)
+        ]
+
+    def up_tile(i, _):
+        slot = lax.rem(i, 2)
+        col = pl.ds(pl.multiple_of(i * 256, 256), 256)
+
+        @pl.when(i >= 2)
+        def _():
+            for c in up_copy(i, slot):
+                c.wait()
+
+        res = dot(xc[0, :, col], grd[...], TN)
+        for e in range(local):
+            gtile[slot, e] = res[:, e * ff : (e + 1) * ff].astype(BF16)
+        for c in up_copy(i, slot):
+            c.start()
+        return 0
+
+    def down_copy(i, slot):
+        return pltpu.make_async_copy(dtile.at[slot], gdn_ref.at[pl.ds(i * 256, 256), :], dsem.at[slot])
+
+    def down_tile(i, _):
+        slot = lax.rem(i, 2)
+        col = pl.ds(pl.multiple_of(i * 256, 256), 256)
+
+        @pl.when(i >= 2)
+        def _():
+            down_copy(i, slot).wait()
+
+        dtile[slot] = dot(hid[:, col], xc[1], TN).astype(BF16)
+        down_copy(i, slot).start()
+        return 0
+
+    n_up, n_down = width // 256, lff // 256
+    tiles = n_up + n_down
+
+    def filler(t):
+        lo, hi = tiles * t // half, tiles * (t + 1) // half
+        if lo < min(hi, n_up):
+            lax.fori_loop(lo, min(hi, n_up), up_tile, 0)
+        if max(lo, n_up) < hi:
+            lax.fori_loop(max(lo, n_up) - n_up, hi - n_up, down_tile, 0)
+
+    for t in range(half):
+        dist = half - t
+        rel = [dist, n - dist]
+        if t == 0:
+            sib_part(half)
+            for d in (0, 1):
+                rss[d, 0, :, cols[d]] = base_sum(half, d).astype(BF16)
+                xsum(d, 1, d).start()
+        else:
+            for d in (0, 1):
+                sib_part(rel[d])
+            for step in (0, 1):
+                for d in (0, 1):
+                    c = (1 - d) if step == 0 else d
+                    total = base_sum(rel[d], c)
+                    if t > 1 or c == d:
+                        xsum(d, t, c).wait_recv()
+                        total = total + rsr[d, t - 1, :, cols[c]].astype(F32)
+                    rss[d, t, :, cols[c]] = total.astype(BF16)
+                    xsum(d, t + 1, c).start()
+        filler(t)
+    sib_part(0)
+    done = []
+    for c in (0, 1):
+        for d in (0, 1):
+            xsum(d, half, c).wait_recv()
+        total = base_sum(0, c) + rsr[0, half - 1, :, cols[c]].astype(F32) + rsr[1, half - 1, :, cols[c]].astype(F32)
+        fin[:, cols[c]] = total.astype(BF16)
+        last = remote(
+            fin.at[:, cols[c]], out_ref.at[:, cols[c]], y_s.at[1 + c], y_r.at[1 + c], (sec_to, me)
+        )
+        last.start()
+        done.append(last)
+
+    cot.wait_send()
+    for d in (0, 1):
+        for s in range(1, half + 1):
+            for piece in (0, 1):
+                if s < half or piece == d:
+                    ring(xc.at[piece, rows(me)], piece, me, d, s).wait_send()
+    for r in range(n):
+        for piece in (0, 1):
+            side(xc.at[piece, rows(me)], piece, me, r).wait_send()
+        remote(sibsend.at[r], sibrecv.at[r], ps_s.at[r], ps_r.at[r], here(sib)).wait_send()
+
+    def told(i, _):
+        to = lax.rem(me + i, ep)
+        remote(idt_ref, idt.at[me], id_s.at[i], id_r.at[me], here(to)).wait_send()
+        remote(paysend.at[to], pay.at[me], pay_s.at[i], pay_r.at[me], here(to)).wait_send()
+        return 0
+
+    lax.fori_loop(1, ep, told, 0)
+    for d in (0, 1):
+        for t in range(half):
+            for c in (0, 1):
+                if t > 0 or c == d:
+                    xsum(d, t + 1, c).wait_send()
+    for slot in range(min(2, n_up)):
+        for c in up_copy(slot, slot):
+            c.wait()
+    for slot in range(min(2, n_down)):
+        down_copy(slot, slot).wait()
+    for c in done:
+        c.wait()
+
+
+def fused_body(ns, ep, inputs, upstream, gate_saved, expert_ids, route_weights, w_up, w_down):
+    toks, top = expert_ids.shape[1:]
+    local, width, ff = w_up.shape[1:]
+    experts = local * ep
+    cap = 3 * toks * top // (2 * experts)
+    n, half = ep // 2, ep // 4
+    lff, lcap = local * ff, local * cap
+    flat = toks * top
+    lanes = 256
+    ids = expert_ids[0].astype(F32)
+    idr = ids.reshape(flat // lanes, lanes)
+    wr = route_weights[0].reshape(flat // lanes, lanes)
+    idt = ids.T
+    hbm = pl.BlockSpec(memory_space=pl.ANY)
+    vmem = pl.BlockSpec(memory_space=pltpu.VMEM)
+    dma = pltpu.SemaphoreType.DMA
+    out, gup, gdn = pl.pallas_call(
+        functools.partial(kernel, ns, ep, toks, top, width, ff, local, cap),
+        out_shape=(
+            jax.ShapeDtypeStruct((toks, width), BF16),
+            jax.ShapeDtypeStruct((local, width, ff), BF16),
+            jax.ShapeDtypeStruct((lff, width), BF16),
+        ),
+        in_specs=[hbm] * 5 + [vmem] * 3,
+        out_specs=(hbm, hbm, hbm),
+        scratch_shapes=[
+            pltpu.VMEM((2, ep * toks, width), BF16),
+            pltpu.VMEM((ep, lcap, ff), BF16),
+            pltpu.VMEM((ep, lcap, ff), BF16),
+            pltpu.VMEM((ep, top, toks), F32),
+            pltpu.VMEM((flat, ff), BF16),
+            pltpu.VMEM((flat, ff), BF16),
+            pltpu.VMEM((flat // lanes, lanes), F32),
+            pltpu.VMEM((width, lff), BF16),
+            pltpu.VMEM((lff, width), BF16),
+            pltpu.VMEM((2 * toks, lff), F32),
+            pltpu.VMEM((ep * toks, lff), BF16),
+            pltpu.VMEM((ep * toks, lff), BF16),
+            pltpu.VMEM((2 * toks, width), F32),
+            pltpu.VMEM((n, toks, width), F32),
+            pltpu.VMEM((n, toks, width), BF16),
+            pltpu.VMEM((n, toks, width), BF16),
+            pltpu.VMEM((2, half, toks, width), BF16),
+            pltpu.VMEM((2, half, toks, width), BF16),
+            pltpu.VMEM((toks, width), BF16),
+            pltpu.VMEM((2, local, 256, ff), BF16),
+            pltpu.VMEM((2, 256, width), BF16),
+            dma((4 * (half + 1),)),
+            dma((4 * (half + 1),)),
+            dma((2 * n,)),
+            dma((2 * n,)),
+            dma((ep,)),
+            dma((ep,)),
+            dma((ep,)),
+            dma((ep,)),
+            dma((n,)),
+            dma((n,)),
+            dma((4 * (half + 1),)),
+            dma((4 * (half + 1),)),
+            dma((3,)),
+            dma((3,)),
+            dma((3 + local,)),
+            dma((2 * local,)),
+            dma((2,)),
+        ],
+        compiler_params=pltpu.CompilerParams(
+            collective_id=0, has_side_effects=True, vmem_limit_bytes=VMEM_BYTES
+        ),
+    )(
+        inputs[0], upstream[0], gate_saved[0].reshape(flat, ff), w_up[0],
+        w_down[0].reshape(lff, width), idr, wr, idt,
+    )
+    return out[None], gup[None], gdn.reshape(1, local, ff, width)
 
 
 def from_behind(block, axis, distance):
@@ -13,7 +444,7 @@
     return lax.ppermute(block, axis, route)
 
 
-def body(inputs, upstream, gate_saved, expert_ids, route_weights, w_up, w_down):
+def plain_body(inputs, upstream, gate_saved, expert_ids, route_weights, w_up, w_down):
     ep = lax.axis_size("ep")
     local = w_up.shape[1]
     experts = local * ep
@@ -51,26 +482,19 @@
     spread = (ranks[:, :, :, None] == jnp.arange(cap).astype(F32)).astype(BF16)
     gate = jnp.einsum("stec,secf->stef", spread, gate_recv, preferred_element_type=F32)
     act = jax.nn.silu(gate).reshape(ep * toks, local, ff)
-    weight = weight.reshape(ep * toks, local, 1)
-    act_w = (act * weight)
-
-    up = w_up[0]
-    down = w_down[0]
-    up_cat = jnp.transpose(up, (1, 0, 2)).reshape(width, local * ff)
-    down_cat = down.reshape(local * ff, width)
-    act_w = act_w.reshape(ep * toks, local * ff)
+    act_w = (act * weight.reshape(ep * toks, local, 1)).reshape(ep * toks, local * ff)
+
+    up_cat = jnp.transpose(w_up[0], (1, 0, 2)).reshape(width, local * ff)
+    down_cat = w_down[0].reshape(local * ff, width)
     u = jnp.dot(x_all, up_cat, preferred_element_type=F32)
     hidden = (act_w * u).astype(BF16)
-    h = lax.dot_general(c_all, down_cat, (((1,), (1,)), ((), ())), preferred_element_type=F32)
+    h = dot(c_all, down_cat, NT)
     g = (act_w * h).astype(BF16)
-    part = lax.dot_general(g, up_cat, (((1,), (1,)), ((), ())), preferred_element_type=F32)
+    part = dot(g, up_cat, NT)
     grad = lax.psum_scatter(part.astype(BF16), "ep", scatter_dimension=0, tiled=True)
     delivered = from_behind(grad[None], "section", -1)
-    grad_down = lax.dot_general(hidden, c_all, (((0,), (0,)), ((), ())), preferred_element_type=F32)
-    grad_up = jnp.stack([
-        lax.dot_general(x_all, g[:, e * ff:(e + 1) * ff], (((0,), (0,)), ((), ())), preferred_element_type=F32)
-        for e in range(local)
-    ])
+    grad_down = dot(hidden, c_all, TN)
+    grad_up = jnp.stack([dot(x_all, g[:, e * ff : (e + 1) * ff], TN) for e in range(local)])
     return (
         delivered,
         grad_up.astype(BF16)[None],
@@ -79,6 +503,17 @@
 
 
 def solution(mesh):
+    ns, ep = mesh.shape["section"], mesh.shape["ep"]
+
+    def body(*args):
+        toks, width = args[0].shape[1:]
+        local, ff = args[5].shape[1], args[5].shape[3]
+        rows = ep * toks
+        need = rows * (4 * width + 4 * local * ff) + 12 * rows * width // 2 + 4 * local * ff * width
+        if need < 0.75 * VMEM_BYTES and ep % 4 == 0:
+            return fused_body(ns, ep, *args)
+        return plain_body(*args)
+
     return jax.shard_map(
         body,
         mesh=mesh,

time: 274 us -> 154 us (0.56)
  Pallas kernels: 0 us -> 143 us
  waiting for transfers between devices: 91.5 us -> 0 us
  matrix products: 69.7 us -> 0 us
  blocking collectives: 45 us -> 0 us
  local copies, waits for them, and re-layouts: 37.8 us -> 8.9 us
  between operations: 13.9 us -> 0.64 us
  starting transfers between devices: 10.8 us -> 0 us
    pallas_call x0 -> x1, Pallas kernels: none -> 143 us  [fused_body(): pl.pallas_call(functools.partial(kernel, ns, ep, toks, top, width, ff, lo...]
    dot_general x9 -> x0, matrix products: 69.7 us -> none  [the longest x1 30.7 us: body(): lax.dot_general(hidden, c_all, (((0,), (0,)), ((), ())), preferred_elemen...]
    reduce_scatter x1 -> x0, waiting for transfers between devices: 51.1 us -> none  [body(): lax.psum_scatter(part.astype(BF16), 'ep', scatter_dimension=0, tiled=True)]
    all_gather x1 -> x0, blocking collectives: 45 us -> none  [body(): routing_all = lax.all_gather(routing, 'ep', axis=0, tiled=False)]
    all_gather x2 -> x0, waiting for transfers between devices: 30.3 us -> none  [the longest x1 30.3 us: body(): x_all = lax.all_gather(inputs[0], 'ep', axis=0, tiled=True)]
    unnamed x22 -> x6, local copies, waits for them, and re-layouts: 21.9 us -> 7.42 us
    reshape x1 -> x0, local copies, waits for them, and re-layouts: 10.3 us -> none  [body(): act = jax.nn.silu(gate).reshape(ep * toks, local, ff)]
    ppermute x2 -> x0, waiting for transfers between devices: 9.33 us -> none  [from_behind(): return lax.ppermute(block, axis, route)]
  transfers between devices with their start and end apart: 6 -> 0, of which waited for: 3 -> 0; matrix products, arithmetic and copies ran while one was open for 39% -> 0% of each run, Pallas kernels for 0% -> 0%
where the time goes in v1:
time: 154 us
  Pallas kernels  143 us (93%)
  local copies, waits for them, and re-layouts  8.9 us (6%)
    pallas_call x1, Pallas kernels, fused_body(): pl.pallas_call(functools.partial(kernel, ns, ep, toks, top, width, ff, lo...  143 us
    unnamed x6, local copies, waits for them, and re-layouts  7.42 us

profile of v1, /device:TPU:0, one launch (start us, length us, event | category | flops | bytes accessed | tf_op | source)
XLA Modules:
  0.0 154.0 jit_solution(229847105905284857)
XLA Ops:
  0.6 1.3 convert_bitcast_fusion
  1.9 0.1 copy.11
  2.0 0.7 convert_element_type.11.idr_ref
  2.7 0.8 copy.12
  3.5 0.7 reshape_squeeze.11.wr_ref
  4.2 143.2 %shard_map.94 = (bf16[128,1536]{1,0:T(8,128)(2,1)}, bf16[2,1536,384]{2,1,0:T(8,128)(2,1)}, bf16[768,1536]{1,0:T(8,128)(2,1)}) custom-call(bf16[128,1536]{1,0:T(8,128)(2,1)} %bitcast.18, bf16[128,1536]{1,0:T(8,128)(2,1)} %bitcast.19, bf16[1024,384]{1,0:T(8,128)(2,1)} %bitcast.16, bf16[2,1536,384]{2,1,0:T(8,128)(2,1)} %bitcast.12, bf16[768,1536]{1,0:T(8,128)(2,1)} %bitcast.13, ...), custom_call_target="tpu_custom_call" | custom-call | tf_op jit(solution)/shard_map/pallas_call | solution.py:382
  147.4 1.8 %copy.16 = bf16[1,128,1536]{2,1,0:T(8,128)(2,1)} copy(bf16[1,128,1536]{2,1,0:T(8,128)(2,1)} %bitcast.17) | data formatting | bytes 786432
  149.2 0.0 copy-start
  149.2 3.5 %copy.17 = bf16[1,2,1536,384]{3,2,1,0:T(8,128)(2,1)} copy(bf16[1,2,1536,384]{3,2,1,0:T(8,128)(2,1)} %bitcast.15) | data formatting | bytes 4718592
  152.6 0.0 copy-done
  152.6 1.4 copy.18
Async XLA Ops:
  149.2 3.5 %copy-start = (bf16[768,1536]{1,0:T(8,128)(2,1)S(1)}, bf16[768,1536]{1,0:T(8,128)(2,1)}, u32[]{:S(2)}) copy-start(bf16[768,1536]{1,0:T(8,128)(2,1)} %get-tuple-element.8) | copy-start | bytes 7077892

commit v2 on v1

--- a/solution.py
+++ b/solution.py
@@ -10,7 +10,7 @@
 BF16 = jnp.bfloat16
 F32 = jnp.float32
 MESH = pl.DeviceIdType.MESH
-VMEM_BYTES = 67_000_000
+VMEM_BYTES = 58_000_000
 TN = (((0,), (0,)), ((), ()))
 NT = (((1,), (1,)), ((), ()))
 
@@ -25,12 +25,12 @@
 
 def kernel(
     ns, ep, toks, top, width, ff, local, cap,
-    x_in, up_in, gate_in, wup_in, wdn_in, idr_ref, wr_ref, idt_ref,
+    x_in, up_in, gate_in, wup_in, wdn_in, idt_ref, wt_ref,
     out_ref, gup_ref, gdn_ref,
-    xc, pay, paysend, idt, gate, act, slots, wup, wdn, dense, hid, grd, part,
-    own, sibsend, sibrecv, rss, rsr, fin, gtile, dtile,
-    ring_s, ring_r, sib_s, sib_r, pay_s, pay_r, id_s, id_r, ps_s, ps_r, rs_s, rs_r,
-    y_s, y_r, loc, gsem, dsem,
+    xc, pay, paysend, idt, gate, act, slots, wflat, wup, wdn, dense, hid, grd, part,
+    own, sibsend, sibrecv, rss, rsr, fin, finr,
+    ring_s, ring_r, col_s, row_s, cot_r, sib_s, sib_r, pay_s, pay_r, id_s, id_r, ps_s, ps_r, rs_s, rs_r,
+    y_s, y_r, loc,
 ):
     n = ep // 2
     half = n // 2
@@ -41,7 +41,9 @@
     sib = me + 1 - 2 * core
     a, b = lax.div(chip, 2), lax.rem(chip, 2)
     pos = (1 - b) * a + b * (n - 1 - a)
-    w2 = width // 2
+    w2, w4 = width // 2, width // 4
+    cols = [slice(0, w2), slice(w2, width)]
+    quarters = [slice(c * w4, (c + 1) * w4) for c in range(4)]
     lff = local * ff
     lcap = local * cap
     two = 2 * toks
@@ -66,7 +68,8 @@
     sec_from = lax.rem(sec + 1, ns)
 
     bar = pltpu.get_barrier_semaphore()
-    greet = [(sec_to, me)] + ([(sec_from, me)] if ns > 2 else [])
+    across = [me] + nxt
+    greet = [(sec_to, dev) for dev in across] + ([(sec_from, dev) for dev in across] if ns > 2 else [])
 
     def hello(i, _):
         pl.semaphore_signal(bar, inc=1, device_id=here(lax.rem(me + i, ep)), device_id_type=MESH)
@@ -87,22 +90,41 @@
         c.start()
     pl.semaphore_wait(bar, ep - 1 + len(greet))
 
-    def ridx(d, s, piece):
-        return (d * (half + 1) + s) * 2 + piece
-
-    def ring(src, piece, dev, d, s):
-        i = ridx(d, s, piece)
-        return remote(src, xc.at[piece, rows(dev)], ring_s.at[i], ring_r.at[i], here(nxt[d]))
-
-    def side(src, piece, dev, r):
-        i = r * 2 + piece
+    def ring(src, dev, d, s):
+        i = d * (half + 1) + s
+        return remote(src, xc.at[0, rows(dev)], ring_s.at[i], ring_r.at[i], here(nxt[d]))
+
+    def ring_last(dev, d):
+        ref = xc.at[0, rows(dev), cols[d]]
+        i = d * (half + 1) + half
+        return remote(ref, ref, ring_s.at[i], ring_r.at[i], here(nxt[d]))
+
+    def side(src, piece, q, dev):
+        i = q * 2 + piece
         return remote(src, xc.at[piece, rows(dev)], sib_s.at[i], sib_r.at[i], here(sib))
+
+    def column(owner, s, d):
+        ref = xc.at[1, rows((owner * 2 + b) * 2 + core)]
+        to = ((a + 1 - 2 * d) * 2 + b) * 2 + core
+        return remote(ref, ref, col_s.at[d * half + s], cot_r.at[owner * 2 + b], here(to))
+
+    def row(owner):
+        ref = xc.at[1, rows((owner * 2 + b) * 2 + core)]
+        to = (a * 2 + 1 - b) * 2 + core
+        return remote(ref, ref, row_s.at[owner], cot_r.at[owner * 2 + b], here(to))
+
+    def cot_arrive(q):
+        ref = xc.at[1, rows(q * 2 + core)]
+        remote(ref, ref, row_s.at[0], cot_r.at[q], here(sib)).wait_recv()
+
+    def cot_side(q):
+        return side(xc.at[1, rows(q * 2 + core)], 1, q, q * 2 + core)
 
     cot = remote(up_in, xc.at[1, rows(me)], y_s.at[0], y_r.at[0], (sec_to, me))
     cot.start()
     for d in (0, 1):
-        ring(x_in, 0, me, d, 1).start()
-    side(x_in, 0, me, 0).start()
+        ring(x_in, me, d, 1).start()
+    side(x_in, 0, chip, me).start()
     idt[me] = idt_ref[...]
 
     def tell(i, _):
@@ -113,11 +135,19 @@
     lax.fori_loop(1, ep, tell, 0)
 
     experts = ep * local
-    lanes = idr_ref.shape[1]
+    lanes = 256
+    parts = toks * top // lanes
+    span = lanes // top
     tri = (iota((lanes, lanes), 0) < iota((lanes, lanes), 1)).astype(BF16)
     base = jnp.zeros((experts, 1), F32)
-    for k in range(idr_ref.shape[0]):
-        ids = idr_ref[k : k + 1, :]
+    ids_t = idt_ref[...].astype(F32).astype(BF16)
+    w_t = wt_ref[...].astype(BF16)
+    mine_k = iota((top, lanes), 0) == lax.rem(iota((top, lanes), 1), top)
+    for k in range(parts):
+        token = lax.div(iota((toks, lanes), 1), top) + k * span
+        take = (iota((toks, lanes), 0) == token).astype(BF16)
+        ids = jnp.sum(jnp.where(mine_k, dot(ids_t, take), 0.0), axis=0, keepdims=True)
+        wflat[k : k + 1, :] = jnp.sum(jnp.where(mine_k, dot(w_t, take), 0.0), axis=0, keepdims=True)
         hot = (iota((experts, lanes), 0).astype(F32) == ids).astype(F32)
         cum = dot(hot.astype(BF16), tri) + base
         base = base + jnp.sum(hot, axis=1, keepdims=True)
@@ -131,14 +161,14 @@
         act[r, :] = (v / (1.0 + jnp.exp(-v))).astype(BF16)
         return 0
 
-    lax.fori_loop(0, idr_ref.shape[0], silu_rows, 0)
+    lax.fori_loop(0, parts, silu_rows, 0)
     group = 4 * lcap
 
     def pack(m, _):
         acc = jnp.zeros((group, ff), F32)
         at = (iota((group, lanes), 0) + m * group).astype(F32)
-        for k in range(idr_ref.shape[0]):
-            pick = jnp.where(at == slots[k : k + 1, :], wr_ref[k : k + 1, :], 0.0).astype(BF16)
+        for k in range(parts):
+            pick = jnp.where(at == slots[k : k + 1, :], wflat[k : k + 1, :], 0.0).astype(BF16)
             acc = acc + dot(pick, act[k * lanes : (k + 1) * lanes, :])
         for j in range(4):
             paysend[m * 4 + j] = acc[j * lcap : (j + 1) * lcap].astype(BF16)
@@ -154,23 +184,28 @@
     lax.fori_loop(1, ep, give, 0)
     pay[me] = paysend[me]
 
+    def reaches(d):
+        return (a + 1 < half) if d == 0 else (a >= 1)
+
     cot.wait_recv()
     for d in (0, 1):
-        ring(xc.at[1, rows(me)], 1, me, d, 1).start()
-    side(xc.at[1, rows(me)], 1, me, 0).start()
+
+        @pl.when(reaches(d))
+        def _():
+            column(a, 0, d).start()
+
+    row(a).start()
+    cot_side(chip).start()
     for c in [local_copies[0]] + local_copies[2:]:
         c.wait()
 
     upper = (iota((toks, toks), 0) < iota((toks, toks), 1)).astype(BF16)
-
-    def arrive(piece, dev, d, s):
-        ring(xc.at[piece, rows(dev)], piece, dev, d, s).wait_recv()
 
     def chunk(r):
         q = chip_at(lax.rem(pos + r, n))
         other = q * 2 + 1 - core
         for piece in (0, 1):
-            side(xc.at[piece, rows(other)], piece, other, r).wait_recv()
+            side(xc.at[piece, rows(other)], piece, q, other).wait_recv()
         for j in (0, 1):
             src = q * 2 + j
 
@@ -181,8 +216,7 @@
 
             names = idt[src]
             for e in range(local):
-                mine = (me * local + e).astype(F32)
-                member = jnp.sum((names == mine).astype(F32), axis=0, keepdims=True)
+                member = jnp.sum((names == me * local + e).astype(F32), axis=0, keepdims=True)
                 rank = dot(jnp.broadcast_to(member, (8, toks)).astype(BF16), upper)[0:1, :]
                 key = jnp.where(member > 0.0, rank, -1.0)
                 spread = (iota((cap, toks), 0).astype(F32) == key).astype(BF16)
@@ -200,91 +234,127 @@
         remote(sibsend.at[r], sibrecv.at[r], ps_s.at[r], ps_r.at[r], here(sib)).start()
         own[r] = part[pl.ds(pl.multiple_of(core * toks, toks), toks), :]
 
+    def hop(d, t, c):
+        i = (d * (half + 1) + t) * 4 + c
+        ref = quarters[c]
+        to = (sec_to, nxt[d]) if t == half else here(nxt[d])
+        return remote(rss.at[d, t - 1, :, ref], rsr.at[d, t - 1, :, ref], rs_s.at[i], rs_r.at[i], to)
+
+    def sib_part(r):
+        remote(sibsend.at[r], sibrecv.at[r], ps_s.at[r], ps_r.at[r], here(sib)).wait_recv()
+
+    def send_sum(t, side_of, first):
+        for j in (0, 1):
+            for d in (0, 1):
+                c = 2 * (d if side_of == 0 else 1 - d) + j
+                r = (half - t) if d == 0 else n - (half - t)
+                total = own[r, :, quarters[c]] + sibrecv[r, :, quarters[c]].astype(F32)
+                if not first:
+                    hop(d, t, c).wait_recv()
+                    total = total + rsr[d, t - 1, :, quarters[c]].astype(F32)
+                rss[d, t, :, quarters[c]] = total.astype(BF16)
+                hop(d, t + 1, c).start()
+
+    def early(t):
+        for d in (0, 1):
+            sib_part((half - t) if d == 0 else n - (half - t))
+        send_sum(t, 1, t == 1)
+
+    own_part = remote(fin, finr, y_s.at[1], y_r.at[1], (sec_to, me))
+
+    last = 2 * half - 2
+
     def event(it, _):
         s = lax.div(it, 2) + 1
-        piece = lax.rem(it, 2)
-
-        @pl.when(it < 2 * (half - 1))
+        turn = lax.rem(it, 2)
+
+        @pl.when((it < last) & (turn == 0))
         def _():
             for d in (0, 1):
-                r = (n - s) if d == 0 else s
-                dev = chip_at(lax.rem(pos + r, n)) * 2 + core
-                arrive(piece, dev, d, s)
-                src = xc.at[piece, rows(dev)]
-
-                @pl.when((s + 1 < half) | (piece == d))
+                q = chip_at(lax.rem(pos + ((n - s) if d == 0 else s), n))
+                dev = q * 2 + core
+                src = xc.at[0, rows(dev)]
+                ring(src, dev, d, s).wait_recv()
+
+                @pl.when(s + 1 < half)
                 def _():
-                    ring(src, piece, dev, d, s + 1).start()
-
-                side(src, piece, dev, r).start()
-
-        @pl.when(it == 2 * half)
+                    ring(src, dev, d, s + 1).start()
+
+                @pl.when(s + 1 == half)
+                def _():
+                    ring_last(dev, d).start()
+
+                side(src, 0, q, dev).start()
+
+        def from_row(owner):
+            @pl.when((owner >= 0) & (owner < half))
+            def _():
+                q = owner * 2 + 1 - b
+                cot_arrive(q)
+                cot_side(q).start()
+
+        @pl.when((it < last) & (turn == 1))
         def _():
             for d in (0, 1):
-                dev = chip_at(lax.rem(pos + half, n)) * 2 + core
-                arrive(d, dev, d, half)
-                side(xc.at[d, rows(dev)], d, dev, half).start()
-
-        @pl.when(it != 1)
+                owner = a - s + 2 * s * d
+
+                @pl.when((owner >= 0) & (owner < half))
+                def _():
+                    q = owner * 2 + b
+                    cot_arrive(q)
+
+                    @pl.when(reaches(d))
+                    def _():
+                        column(owner, s, d).start()
+
+                    row(owner).start()
+                    cot_side(q).start()
+
+            from_row(a + s - 1)
+
+            @pl.when(s > 1)
+            def _():
+                from_row(a - s + 1)
+
+        @pl.when(it == 2)
         def _():
-            dist = lax.div(it, 2)
-            chunk((1 - piece) * dist + piece * (n - dist))
-
-        return 0
-
-    lax.fori_loop(0, 2 * half + 1, event, 0)
-
-    cols = [slice(0, w2), slice(w2, width)]
-
-    def xsum(d, t, c):
-        i = (d * (half + 1) + t) * 2 + c
-        return remote(
-            rss.at[d, t - 1, :, cols[c]], rsr.at[d, t - 1, :, cols[c]], rs_s.at[i], rs_r.at[i], here(nxt[d])
-        )
-
-    def sib_part(r):
-        remote(sibsend.at[r], sibrecv.at[r], ps_s.at[r], ps_r.at[r], here(sib)).wait_recv()
-
-    def base_sum(r, c):
-        return own[r, :, cols[c]] + sibrecv[r, :, cols[c]].astype(F32)
-
-    def up_copy(i, slot):
-        return [
-            pltpu.make_async_copy(
-                gtile.at[slot, e], gup_ref.at[e, pl.ds(i * 256, 256), :], gsem.at[slot * local + e]
-            )
-            for e in range(local)
-        ]
+            sib_part(0)
+            fin[...] = (own[0] + sibrecv[0].astype(F32)).astype(BF16)
+            own_part.start()
+
+        @pl.when(it == last)
+        def _():
+            early(1)
+            q = chip_at(lax.rem(pos + half, n))
+            dev = q * 2 + core
+            for d in (0, 1):
+                ring_last(dev, d).wait_recv()
+            side(xc.at[0, rows(dev)], 0, q, dev).start()
+            from_row(a + half - 1)
+            from_row(a - half + 1)
+
+        away = s * jnp.minimum(it, 1)
+
+        def compute(j, _):
+            chunk(away + j * (n - 2 * away))
+            return 0
+
+        ends = (it == 0).astype(jnp.int32) + (it == last).astype(jnp.int32)
+        lax.fori_loop(0, 2 * turn + ends, compute, 0)
+        return 0
+
+    lax.fori_loop(0, last + 1, event, 0)
 
     def up_tile(i, _):
-        slot = lax.rem(i, 2)
         col = pl.ds(pl.multiple_of(i * 256, 256), 256)
-
-        @pl.when(i >= 2)
-        def _():
-            for c in up_copy(i, slot):
-                c.wait()
-
         res = dot(xc[0, :, col], grd[...], TN)
         for e in range(local):
-            gtile[slot, e] = res[:, e * ff : (e + 1) * ff].astype(BF16)
-        for c in up_copy(i, slot):
-            c.start()
-        return 0
-
-    def down_copy(i, slot):
-        return pltpu.make_async_copy(dtile.at[slot], gdn_ref.at[pl.ds(i * 256, 256), :], dsem.at[slot])
+            gup_ref[e, col, :] = res[:, e * ff : (e + 1) * ff].astype(BF16)
+        return 0
 
     def down_tile(i, _):
-        slot = lax.rem(i, 2)
         col = pl.ds(pl.multiple_of(i * 256, 256), 256)
-
-        @pl.when(i >= 2)
-        def _():
-            down_copy(i, slot).wait()
-
-        dtile[slot] = dot(hid[:, col], xc[1], TN).astype(BF16)
-        down_copy(i, slot).start()
+        gdn_ref[col, :] = dot(hid[:, col], xc[1], TN).astype(BF16)
         return 0
 
     n_up, n_down = width // 256, lff // 256
@@ -297,49 +367,42 @@
         if max(lo, n_up) < hi:
             lax.fori_loop(max(lo, n_up) - n_up, hi - n_up, down_tile, 0)
 
+    sib_part(half)
     for t in range(half):
-        dist = half - t
-        rel = [dist, n - dist]
-        if t == 0:
-            sib_part(half)
+        send_sum(t, 0, t == 0)
+        filler(t)
+        if t + 2 < half:
+            early(t + 2)
+    own_part.wait_recv()
+    for part_of in (1, 0):
+        for j in (0, 1):
             for d in (0, 1):
-                rss[d, 0, :, cols[d]] = base_sum(half, d).astype(BF16)
-                xsum(d, 1, d).start()
-        else:
-            for d in (0, 1):
-                sib_part(rel[d])
-            for step in (0, 1):
-                for d in (0, 1):
-                    c = (1 - d) if step == 0 else d
-                    total = base_sum(rel[d], c)
-                    if t > 1 or c == d:
-                        xsum(d, t, c).wait_recv()
-                        total = total + rsr[d, t - 1, :, cols[c]].astype(F32)
-                    rss[d, t, :, cols[c]] = total.astype(BF16)
-                    xsum(d, t + 1, c).start()
-        filler(t)
-    sib_part(0)
-    done = []
-    for c in (0, 1):
-        for d in (0, 1):
-            xsum(d, half, c).wait_recv()
-        total = base_sum(0, c) + rsr[0, half - 1, :, cols[c]].astype(F32) + rsr[1, half - 1, :, cols[c]].astype(F32)
-        fin[:, cols[c]] = total.astype(BF16)
-        last = remote(
-            fin.at[:, cols[c]], out_ref.at[:, cols[c]], y_s.at[1 + c], y_r.at[1 + c], (sec_to, me)
-        )
-        last.start()
-        done.append(last)
+                c = 2 * (d if part_of == 0 else 1 - d) + j
+                hop(d, half, c).wait_recv()
+                got = rsr[d, half - 1, :, quarters[c]].astype(F32)
+                if part_of == 1:
+                    own[0, :, quarters[c]] = finr[:, quarters[c]].astype(F32) + got
+                else:
+                    out_ref[:, quarters[c]] = (own[0, :, quarters[c]] + got).astype(BF16)
 
     cot.wait_send()
+    own_part.wait_send()
     for d in (0, 1):
-        for s in range(1, half + 1):
-            for piece in (0, 1):
-                if s < half or piece == d:
-                    ring(xc.at[piece, rows(me)], piece, me, d, s).wait_send()
+        for s in range(1, half):
+            ring(xc.at[0, rows(me)], me, d, s).wait_send()
+        ring_last(me, d).wait_send()
+        for s in range(half):
+            owner = a - s + 2 * s * d
+
+            @pl.when(reaches(d) & (owner >= 0) & (owner < half))
+            def _():
+                column(owner, s, d).wait_send()
+
+    for owner in range(half):
+        row(owner).wait_send()
     for r in range(n):
         for piece in (0, 1):
-            side(xc.at[piece, rows(me)], piece, me, r).wait_send()
+            side(xc.at[piece, rows(me)], piece, r, me).wait_send()
         remote(sibsend.at[r], sibrecv.at[r], ps_s.at[r], ps_r.at[r], here(sib)).wait_send()
 
     def told(i, _):
@@ -351,16 +414,9 @@
     lax.fori_loop(1, ep, told, 0)
     for d in (0, 1):
         for t in range(half):
-            for c in (0, 1):
-                if t > 0 or c == d:
-                    xsum(d, t + 1, c).wait_send()
-    for slot in range(min(2, n_up)):
-        for c in up_copy(slot, slot):
-            c.wait()
-    for slot in range(min(2, n_down)):
-        down_copy(slot, slot).wait()
-    for c in done:
-        c.wait()
+            for c in range(4):
+                if t > 0 or c // 2 == d:
+                    hop(d, t + 1, c).wait_send()
 
 
 def fused_body(ns, ep, inputs, upstream, gate_saved, expert_ids, route_weights, w_up, w_down):
@@ -371,31 +427,27 @@
     n, half = ep // 2, ep // 4
     lff, lcap = local * ff, local * cap
     flat = toks * top
-    lanes = 256
-    ids = expert_ids[0].astype(F32)
-    idr = ids.reshape(flat // lanes, lanes)
-    wr = route_weights[0].reshape(flat // lanes, lanes)
-    idt = ids.T
     hbm = pl.BlockSpec(memory_space=pl.ANY)
     vmem = pl.BlockSpec(memory_space=pltpu.VMEM)
     dma = pltpu.SemaphoreType.DMA
     out, gup, gdn = pl.pallas_call(
         functools.partial(kernel, ns, ep, toks, top, width, ff, local, cap),
         out_shape=(
-            jax.ShapeDtypeStruct((toks, width), BF16),
-            jax.ShapeDtypeStruct((local, width, ff), BF16),
-            jax.ShapeDtypeStruct((lff, width), BF16),
+            pltpu.VMEM((toks, width), BF16),
+            pltpu.VMEM((local, width, ff), BF16),
+            pltpu.VMEM((lff, width), BF16),
         ),
-        in_specs=[hbm] * 5 + [vmem] * 3,
-        out_specs=(hbm, hbm, hbm),
+        in_specs=[hbm] * 5 + [vmem] * 2,
+        out_specs=(vmem, vmem, vmem),
         scratch_shapes=[
             pltpu.VMEM((2, ep * toks, width), BF16),
             pltpu.VMEM((ep, lcap, ff), BF16),
             pltpu.VMEM((ep, lcap, ff), BF16),
-            pltpu.VMEM((ep, top, toks), F32),
+            pltpu.VMEM((ep, top, toks), jnp.int32),
             pltpu.VMEM((flat, ff), BF16),
             pltpu.VMEM((flat, ff), BF16),
-            pltpu.VMEM((flat // lanes, lanes), F32),
+            pltpu.VMEM((flat // 256, 256), F32),
+            pltpu.VMEM((flat // 256, 256), F32),
             pltpu.VMEM((width, lff), BF16),
             pltpu.VMEM((lff, width), BF16),
             pltpu.VMEM((2 * toks, lff), F32),
@@ -408,10 +460,12 @@
             pltpu.VMEM((2, half, toks, width), BF16),
             pltpu.VMEM((2, half, toks, width), BF16),
             pltpu.VMEM((toks, width), BF16),
-            pltpu.VMEM((2, local, 256, ff), BF16),
-            pltpu.VMEM((2, 256, width), BF16),
-            dma((4 * (half + 1),)),
-            dma((4 * (half + 1),)),
+            pltpu.VMEM((toks, width), BF16),
+            dma((2 * (half + 1),)),
+            dma((2 * (half + 1),)),
+            dma((2 * half,)),
+            dma((half,)),
+            dma((n,)),
             dma((2 * n,)),
             dma((2 * n,)),
             dma((ep,)),
@@ -420,20 +474,18 @@
             dma((ep,)),
             dma((n,)),
             dma((n,)),
-            dma((4 * (half + 1),)),
-            dma((4 * (half + 1),)),
-            dma((3,)),
-            dma((3,)),
+            dma((8 * (half + 1),)),
+            dma((8 * (half + 1),)),
+            dma((2,)),
+            dma((2,)),
             dma((3 + local,)),
-            dma((2 * local,)),
-            dma((2,)),
         ],
         compiler_params=pltpu.CompilerParams(
             collective_id=0, has_side_effects=True, vmem_limit_bytes=VMEM_BYTES
         ),
     )(
         inputs[0], upstream[0], gate_saved[0].reshape(flat, ff), w_up[0],
-        w_down[0].reshape(lff, width), idr, wr, idt,
+        w_down[0].reshape(lff, width), expert_ids[0].T, route_weights[0].T,
     )
     return out[None], gup[None], gdn.reshape(1, local, ff, width)
 
@@ -510,7 +562,7 @@
         local, ff = args[5].shape[1], args[5].shape[3]
         rows = ep * toks
         need = rows * (4 * width + 4 * local * ff) + 12 * rows * width // 2 + 4 * local * ff * width
-        if need < 0.75 * VMEM_BYTES and ep % 4 == 0:
+        if need < 0.75 * VMEM_BYTES and ep % 8 == 0:
             return fused_body(ns, ep, *args)
         return plain_body(*args)
 

time: 154 us -> 135 us (0.88)
  Pallas kernels: 143 us -> 130 us
  local copies, waits for them, and re-layouts: 8.9 us -> 3.56 us
    pallas_call x1, Pallas kernels: 143 us -> 130 us  [fused_body(): pl.pallas_call(functools.partial(kernel, ns, ep, toks, top, width, ff, lo...]
    unnamed x6 -> x3, local copies, waits for them, and re-layouts: 7.42 us -> 3.56 us
where the time goes in v2:
time: 135 us
  Pallas kernels  130 us (96%)
  local copies, waits for them, and re-layouts  3.56 us (3%)
    pallas_call x1, Pallas kernels, fused_body(): pl.pallas_call(functools.partial(kernel, ns, ep, toks, top, width, ff, lo...  130 us
    unnamed x3, local copies, waits for them, and re-layouts  3.56 us

profile of v2, /device:TPU:0, one launch (start us, length us, event | category | flops | bytes accessed | tf_op | source)
XLA Modules:
  0.0 134.6 jit_solution(4026390687991285927)
XLA Ops:
  0.6 130.4 %shard_map.94 = (bf16[128,1536]{1,0:T(8,128)(2,1)S(1)}, bf16[2,1536,384]{2,1,0:T(8,128)(2,1)S(1)}, bf16[768,1536]{1,0:T(8,128)(2,1)S(1)}) custom-call(bf16[128,1536]{1,0:T(8,128)(2,1)} %bitcast.20, bf16[128,1536]{1,0:T(8,128)(2,1)} %bitcast.21, bf16[1024,384]{1,0:T(8,128)(2,1)} %bitcast.19, bf16[2,1536,384]{2,1,0:T(8,128)(2,1)} %bitcast.17, ...), custom_call_target="tpu_custom_call" | custom-call | tf_op jit(solution)/shard_map/pallas_call | solution.py:433
  131.1 0.7 copy.13
  131.8 1.4 %copy.14 = bf16[1,2,1536,384]{3,2,1,0:T(8,128)(2,1)} copy(bf16[1,2,1536,384]{3,2,1,0:T(8,128)(2,1)S(1)} %bitcast.15) | data formatting | bytes 4718592
  133.2 1.4 %copy.15 = bf16[1,2,384,1536]{3,2,1,0:T(8,128)(2,1)} copy(bf16[1,2,384,1536]{3,2,1,0:T(8,128)(2,1)S(1)} %bitcast.14) | data formatting | bytes 4718592

commit v3 on v2

--- a/solution.py
+++ b/solution.py
@@ -27,10 +27,10 @@
     ns, ep, toks, top, width, ff, local, cap,
     x_in, up_in, gate_in, wup_in, wdn_in, idt_ref, wt_ref,
     out_ref, gup_ref, gdn_ref,
-    xc, pay, paysend, idt, gate, act, slots, wflat, wup, wdn, dense, hid, grd, part,
-    own, sibsend, sibrecv, rss, rsr, fin, finr,
+    xc, pay, paysend, idt, gate, act, slots, wflat, wup, wdn, hid, grd, part,
+    own, sibsend, sibrecv, rss, rsr, fin, finr, over,
     ring_s, ring_r, col_s, row_s, cot_r, sib_s, sib_r, pay_s, pay_r, id_s, id_r, ps_s, ps_r, rs_s, rs_r,
-    y_s, y_r, loc,
+    y_s, y_r, over_s, over_r, loc,
 ):
     n = ep // 2
     half = n // 2
@@ -68,7 +68,7 @@
     sec_from = lax.rem(sec + 1, ns)
 
     bar = pltpu.get_barrier_semaphore()
-    across = [me] + nxt
+    across = [me]
     greet = [(sec_to, dev) for dev in across] + ([(sec_from, dev) for dev in across] if ns > 2 else [])
 
     def hello(i, _):
@@ -201,11 +201,18 @@
 
     upper = (iota((toks, toks), 0) < iota((toks, toks), 1)).astype(BF16)
 
-    def chunk(r):
+    def chunk_of(k):
+        odd = lax.rem(k, 2)
+        r = odd * lax.div(k + 1, 2) + (1 - odd) * lax.rem(n - lax.div(k, 2), n)
         q = chip_at(lax.rem(pos + r, n))
-        other = q * 2 + 1 - core
-        for piece in (0, 1):
-            side(xc.at[piece, rows(other)], piece, q, other).wait_recv()
+        return r, q, pl.ds(pl.multiple_of(q * two, two), two)
+
+    def other_side(piece, q):
+        dev = q * 2 + 1 - core
+        side(xc.at[piece, rows(dev)], piece, q, dev).wait_recv()
+
+    def spread(k, _):
+        r, q, both = chunk_of(k)
         for j in (0, 1):
             src = q * 2 + j
 
@@ -219,46 +226,71 @@
                 member = jnp.sum((names == me * local + e).astype(F32), axis=0, keepdims=True)
                 rank = dot(jnp.broadcast_to(member, (8, toks)).astype(BF16), upper)[0:1, :]
                 key = jnp.where(member > 0.0, rank, -1.0)
-                spread = (iota((cap, toks), 0).astype(F32) == key).astype(BF16)
-                dense[j * toks : (j + 1) * toks, e * ff : (e + 1) * ff] = dot(
-                    spread, pay[src, e * cap : (e + 1) * cap, :], TN
-                )
-        both = pl.ds(pl.multiple_of(q * two, two), two)
-        u = dot(xc[0, both, :], wup[...])
-        hid[both, :] = (dense[...] * u).astype(BF16)
-        h = dot(xc[1, both, :], wdn[...], NT)
-        g = (dense[...] * h).astype(BF16)
+                to_slot = (iota((cap, toks), 0).astype(F32) == key).astype(BF16)
+                grd[rows(src), e * ff : (e + 1) * ff] = dot(
+                    to_slot, pay[src, e * cap : (e + 1) * cap, :], TN
+                ).astype(BF16)
+        return 0
+
+    def stage_x(k, _):
+        r, q, both = chunk_of(k)
+        other_side(0, q)
+        hid[both, :] = (grd[both, :].astype(F32) * dot(xc[0, both, :], wup[...])).astype(BF16)
+        return 0
+
+    def stage_c(k, _):
+        r, q, both = chunk_of(k)
+        other_side(1, q)
+        g = (grd[both, :].astype(F32) * dot(xc[1, both, :], wdn[...], NT)).astype(BF16)
         grd[both, :] = g
         part[...] = dot(g, wup[...], NT)
         sibsend[r] = part[pl.ds(pl.multiple_of((1 - core) * toks, toks), toks), :].astype(BF16)
         remote(sibsend.at[r], sibrecv.at[r], ps_s.at[r], ps_r.at[r], here(sib)).start()
         own[r] = part[pl.ds(pl.multiple_of(core * toks, toks), toks), :]
+        return 0
 
     def hop(d, t, c):
         i = (d * (half + 1) + t) * 4 + c
         ref = quarters[c]
-        to = (sec_to, nxt[d]) if t == half else here(nxt[d])
-        return remote(rss.at[d, t - 1, :, ref], rsr.at[d, t - 1, :, ref], rs_s.at[i], rs_r.at[i], to)
+        src = over.at[d, :, ref] if t == half else rss.at[d, t - 1, :, ref]
+        return remote(src, rsr.at[d, t - 1, :, ref], rs_s.at[i], rs_r.at[i], here(nxt[d]))
+
+    def cross(d, c):
+        i = d * 4 + c
+        ref = quarters[c]
+        return remote(rss.at[d, half - 1, :, ref], over.at[d, :, ref], over_s.at[i], over_r.at[i], (sec_to, me))
+
+    def quarters_of(side_of):
+        return [(d, 2 * (d if side_of == 0 else 1 - d) + j) for j in (0, 1) for d in (0, 1)]
+
+    def pass_on(side_of):
+        for d, c in quarters_of(side_of):
+            cross(d, c).wait_recv()
+            hop(d, half, c).start()
 
     def sib_part(r):
         remote(sibsend.at[r], sibrecv.at[r], ps_s.at[r], ps_r.at[r], here(sib)).wait_recv()
 
-    def send_sum(t, side_of, first):
-        for j in (0, 1):
-            for d in (0, 1):
-                c = 2 * (d if side_of == 0 else 1 - d) + j
-                r = (half - t) if d == 0 else n - (half - t)
-                total = own[r, :, quarters[c]] + sibrecv[r, :, quarters[c]].astype(F32)
-                if not first:
-                    hop(d, t, c).wait_recv()
-                    total = total + rsr[d, t - 1, :, quarters[c]].astype(F32)
-                rss[d, t, :, quarters[c]] = total.astype(BF16)
+    def send_sum(t, side_of, first, ways=(0, 1)):
+        for d, c in [p for p in quarters_of(side_of) if p[0] in ways]:
+            r = (half - t) if d == 0 else n - (half - t)
+            total = own[r, :, quarters[c]] + sibrecv[r, :, quarters[c]].astype(F32)
+            if not first:
+                hop(d, t, c).wait_recv()
+                total = total + rsr[d, t - 1, :, quarters[c]].astype(F32)
+            rss[d, t, :, quarters[c]] = total.astype(BF16)
+            if t + 1 < half:
                 hop(d, t + 1, c).start()
+            else:
+                cross(d, c).start()
 
     def early(t):
         for d in (0, 1):
             sib_part((half - t) if d == 0 else n - (half - t))
-        send_sum(t, 1, t == 1)
+            if t == 1:
+                send_sum(t, 1, True, (d,))
+        if t > 1:
+            send_sum(t, 1, False)
 
     own_part = remote(fin, finr, y_s.at[1], y_r.at[1], (sec_to, me))
 
@@ -324,23 +356,23 @@
 
         @pl.when(it == last)
         def _():
-            early(1)
             q = chip_at(lax.rem(pos + half, n))
             dev = q * 2 + core
             for d in (0, 1):
                 ring_last(dev, d).wait_recv()
             side(xc.at[0, rows(dev)], 0, q, dev).start()
+            early(1)
             from_row(a + half - 1)
             from_row(a - half + 1)
 
-        away = s * jnp.minimum(it, 1)
-
-        def compute(j, _):
-            chunk(away + j * (n - 2 * away))
-            return 0
-
-        ends = (it == 0).astype(jnp.int32) + (it == last).astype(jnp.int32)
-        lax.fori_loop(0, 2 * turn + ends, compute, 0)
+        final = (it == last).astype(jnp.int32)
+        x_lo = (it + jnp.minimum(it, 1)) * (1 - final) + (n - 1) * final
+        x_hi = x_lo + (1 - turn) * ((2 + (it == 0).astype(jnp.int32)) * (1 - final) + final)
+        ahead = (1 - turn) * (1 - final) * (x_hi - x_lo + (it == last - 2).astype(jnp.int32))
+        lax.fori_loop(x_lo, x_lo + ahead, spread, 0)
+        lax.fori_loop(x_lo, x_hi, stage_x, 0)
+        c_lo = it * (1 - final) + (n - 1) * final
+        lax.fori_loop(c_lo, c_lo + 2 * turn + (it == 0).astype(jnp.int32) + final, stage_c, 0)
         return 0
 
     lax.fori_loop(0, last + 1, event, 0)
@@ -358,32 +390,38 @@
         return 0
 
     n_up, n_down = width // 256, lff // 256
-    tiles = n_up + n_down
-
-    def filler(t):
-        lo, hi = tiles * t // half, tiles * (t + 1) // half
-        if lo < min(hi, n_up):
-            lax.fori_loop(lo, min(hi, n_up), up_tile, 0)
-        if max(lo, n_up) < hi:
-            lax.fori_loop(max(lo, n_up) - n_up, hi - n_up, down_tile, 0)
+
+    def fill_up(lo, hi):
+        lax.fori_loop(lo, hi, up_tile, 0)
+
+    def fill_down(lo, hi):
+        lax.fori_loop(lo, hi, down_tile, 0)
 
     sib_part(half)
     for t in range(half):
         send_sum(t, 0, t == 0)
-        filler(t)
+        if t == 1:
+            fill_up(n_up // 2, n_up)
         if t + 2 < half:
             early(t + 2)
+        elif t + 2 == half:
+            pass_on(1)
+        if t == 0:
+            fill_up(0, n_up // 2)
+            fill_down(0, 1)
+        elif t == 1:
+            fill_down(1, 2)
+    fill_down(2, n_down)
+    pass_on(0)
     own_part.wait_recv()
-    for part_of in (1, 0):
-        for j in (0, 1):
-            for d in (0, 1):
-                c = 2 * (d if part_of == 0 else 1 - d) + j
-                hop(d, half, c).wait_recv()
-                got = rsr[d, half - 1, :, quarters[c]].astype(F32)
-                if part_of == 1:
-                    own[0, :, quarters[c]] = finr[:, quarters[c]].astype(F32) + got
-                else:
-                    out_ref[:, quarters[c]] = (own[0, :, quarters[c]] + got).astype(BF16)
+    for side_of in (1, 0):
+        for d, c in quarters_of(side_of):
+            hop(d, half, c).wait_recv()
+            got = rsr[d, half - 1, :, quarters[c]].astype(F32)
+            if side_of == 1:
+                own[0, :, quarters[c]] = finr[:, quarters[c]].astype(F32) + got
+            else:
+                out_ref[:, quarters[c]] = (own[0, :, quarters[c]] + got).astype(BF16)
 
     cot.wait_send()
     own_part.wait_send()
@@ -417,6 +455,8 @@
             for c in range(4):
                 if t > 0 or c // 2 == d:
                     hop(d, t + 1, c).wait_send()
+        for c in range(4):
+            cross(d, c).wait_send()
 
 
 def fused_body(ns, ep, inputs, upstream, gate_saved, expert_ids, route_weights, w_up, w_down):
@@ -450,7 +490,6 @@
             pltpu.VMEM((flat // 256, 256), F32),
             pltpu.VMEM((width, lff), BF16),
             pltpu.VMEM((lff, width), BF16),
-            pltpu.VMEM((2 * toks, lff), F32),
             pltpu.VMEM((ep * toks, lff), BF16),
             pltpu.VMEM((ep * toks, lff), BF16),
             pltpu.VMEM((2 * toks, width), F32),
@@ -461,6 +500,7 @@
             pltpu.VMEM((2, half, toks, width), BF16),
             pltpu.VMEM((toks, width), BF16),
             pltpu.VMEM((toks, width), BF16),
+            pltpu.VMEM((2, toks, width), BF16),
             dma((2 * (half + 1),)),
             dma((2 * (half + 1),)),
             dma((2 * half,)),
@@ -478,6 +518,8 @@
             dma((8 * (half + 1),)),
             dma((2,)),
             dma((2,)),
+            dma((8,)),
+            dma((8,)),
             dma((3 + local,)),
         ],
         compiler_params=pltpu.CompilerParams(

time: 135 us -> 133 us (0.985)
  Pallas kernels: 130 us -> 128 us
    pallas_call x1, Pallas kernels: 130 us -> 128 us  [fused_body(): pl.pallas_call(functools.partial(kernel, ns, ep, toks, top, width, ff, lo...]
where the time goes in v3:
time: 133 us
  Pallas kernels  128 us (96%)
  local copies, waits for them, and re-layouts  3.56 us (3%)
    pallas_call x1, Pallas kernels, fused_body(): pl.pallas_call(functools.partial(kernel, ns, ep, toks, top, width, ff, lo...  128 us
    unnamed x3, local copies, waits for them, and re-layouts  3.56 us

profile of v3, /device:TPU:0, one launch (start us, length us, event | category | flops | bytes accessed | tf_op | source)
XLA Modules:
  0.0 132.6 jit_solution(7996184332589203781)
XLA Ops:
  0.6 128.4 %shard_map.94 = (bf16[128,1536]{1,0:T(8,128)(2,1)S(1)}, bf16[2,1536,384]{2,1,0:T(8,128)(2,1)S(1)}, bf16[768,1536]{1,0:T(8,128)(2,1)S(1)}) custom-call(bf16[128,1536]{1,0:T(8,128)(2,1)} %bitcast.20, bf16[128,1536]{1,0:T(8,128)(2,1)} %bitcast.21, bf16[1024,384]{1,0:T(8,128)(2,1)} %bitcast.19, bf16[2,1536,384]{2,1,0:T(8,128)(2,1)} %bitcast.17, ...), custom_call_target="tpu_custom_call" | custom-call | tf_op jit(solution)/shard_map/pallas_call | solution.py:473
  129.0 0.7 copy.13
  129.7 1.4 %copy.14 = bf16[1,2,1536,384]{3,2,1,0:T(8,128)(2,1)} copy(bf16[1,2,1536,384]{3,2,1,0:T(8,128)(2,1)S(1)} %bitcast.15) | data formatting | bytes 4718592
  131.2 1.4 %copy.15 = bf16[1,2,384,1536]{3,2,1,0:T(8,128)(2,1)} copy(bf16[1,2,384,1536]{3,2,1,0:T(8,128)(2,1)S(1)} %bitcast.14) | data formatting | bytes 4718592

commit v4 on v3

--- a/solution.py
+++ b/solution.py
@@ -99,32 +99,40 @@
         i = d * (half + 1) + half
         return remote(ref, ref, ring_s.at[i], ring_r.at[i], here(nxt[d]))
 
-    def side(src, piece, q, dev):
-        i = q * 2 + piece
-        return remote(src, xc.at[piece, rows(dev)], sib_s.at[i], sib_r.at[i], here(sib))
-
-    def column(owner, s, d):
-        ref = xc.at[1, rows((owner * 2 + b) * 2 + core)]
+    def side(src, q, dev):
+        return remote(src, xc.at[0, rows(dev)], sib_s.at[q * 3], sib_r.at[q * 3], here(sib))
+
+    def cot_ref(q, h, of=core):
+        return xc.at[1, rows(q * 2 + of), cols[h]]
+
+    def column(owner, s, d, h):
+        ref = cot_ref(owner * 2 + b, h)
         to = ((a + 1 - 2 * d) * 2 + b) * 2 + core
-        return remote(ref, ref, col_s.at[d * half + s], cot_r.at[owner * 2 + b], here(to))
-
-    def row(owner):
-        ref = xc.at[1, rows((owner * 2 + b) * 2 + core)]
+        return remote(
+            ref, ref, col_s.at[(d * half + s) * 2 + h], cot_r.at[(owner * 2 + b) * 2 + h], here(to)
+        )
+
+    def row(owner, h):
+        ref = cot_ref(owner * 2 + b, h)
         to = (a * 2 + 1 - b) * 2 + core
-        return remote(ref, ref, row_s.at[owner], cot_r.at[owner * 2 + b], here(to))
-
-    def cot_arrive(q):
-        ref = xc.at[1, rows(q * 2 + core)]
-        remote(ref, ref, row_s.at[0], cot_r.at[q], here(sib)).wait_recv()
-
-    def cot_side(q):
-        return side(xc.at[1, rows(q * 2 + core)], 1, q, q * 2 + core)
-
-    cot = remote(up_in, xc.at[1, rows(me)], y_s.at[0], y_r.at[0], (sec_to, me))
-    cot.start()
+        return remote(ref, ref, row_s.at[owner * 2 + h], cot_r.at[(owner * 2 + b) * 2 + h], here(to))
+
+    def cot_arrive(q, h):
+        ref = cot_ref(q, h)
+        remote(ref, ref, row_s.at[h], cot_r.at[q * 2 + h], here(sib)).wait_recv()
+
+    def cot_side(q, h, of=core):
+        ref = cot_ref(q, h, of)
+        return remote(ref, ref, sib_s.at[q * 3 + 1 + h], sib_r.at[q * 3 + 1 + h], here(sib))
+
+    def cot_in(h):
+        return remote(up_in.at[:, cols[h]], cot_ref(chip, h), y_s.at[h], y_r.at[h], (sec_to, me))
+
+    for h in (0, 1):
+        cot_in(h).start()
     for d in (0, 1):
         ring(x_in, me, d, 1).start()
-    side(x_in, 0, chip, me).start()
+    side(x_in, chip, me).start()
     idt[me] = idt_ref[...]
 
     def tell(i, _):
@@ -187,15 +195,16 @@
     def reaches(d):
         return (a + 1 < half) if d == 0 else (a >= 1)
 
-    cot.wait_recv()
-    for d in (0, 1):
-
-        @pl.when(reaches(d))
-        def _():
-            column(a, 0, d).start()
-
-    row(a).start()
-    cot_side(chip).start()
+    for h in (0, 1):
+        cot_in(h).wait_recv()
+        for d in (0, 1):
+
+            @pl.when(reaches(d))
+            def _():
+                column(a, 0, d, h).start()
+
+        row(a, h).start()
+        cot_side(chip, h).start()
     for c in [local_copies[0]] + local_copies[2:]:
         c.wait()
 
@@ -206,10 +215,6 @@
         r = odd * lax.div(k + 1, 2) + (1 - odd) * lax.rem(n - lax.div(k, 2), n)
         q = chip_at(lax.rem(pos + r, n))
         return r, q, pl.ds(pl.multiple_of(q * two, two), two)
-
-    def other_side(piece, q):
-        dev = q * 2 + 1 - core
-        side(xc.at[piece, rows(dev)], piece, q, dev).wait_recv()
 
     def spread(k, _):
         r, q, both = chunk_of(k)
@@ -234,13 +239,15 @@
 
     def stage_x(k, _):
         r, q, both = chunk_of(k)
-        other_side(0, q)
+        dev = q * 2 + 1 - core
+        side(xc.at[0, rows(dev)], q, dev).wait_recv()
         hid[both, :] = (grd[both, :].astype(F32) * dot(xc[0, both, :], wup[...])).astype(BF16)
         return 0
 
     def stage_c(k, _):
         r, q, both = chunk_of(k)
-        other_side(1, q)
+        for h in (0, 1):
+            cot_side(q, h, 1 - core).wait_recv()
         g = (grd[both, :].astype(F32) * dot(xc[1, both, :], wdn[...], NT)).astype(BF16)
         grd[both, :] = g
         part[...] = dot(g, wup[...], NT)
@@ -292,7 +299,7 @@
         if t > 1:
             send_sum(t, 1, False)
 
-    own_part = remote(fin, finr, y_s.at[1], y_r.at[1], (sec_to, me))
+    own_part = remote(fin, finr, y_s.at[2], y_r.at[2], (sec_to, me))
 
     last = 2 * half - 2
 
@@ -316,31 +323,33 @@
                 def _():
                     ring_last(dev, d).start()
 
-                side(src, 0, q, dev).start()
+                side(src, q, dev).start()
 
         def from_row(owner):
             @pl.when((owner >= 0) & (owner < half))
             def _():
                 q = owner * 2 + 1 - b
-                cot_arrive(q)
-                cot_side(q).start()
+                for h in (0, 1):
+                    cot_arrive(q, h)
+                    cot_side(q, h).start()
 
         @pl.when((it < last) & (turn == 1))
         def _():
-            for d in (0, 1):
-                owner = a - s + 2 * s * d
-
-                @pl.when((owner >= 0) & (owner < half))
-                def _():
-                    q = owner * 2 + b
-                    cot_arrive(q)
-
-                    @pl.when(reaches(d))
+            for h in (0, 1):
+                for d in (0, 1):
+                    owner = a - s + 2 * s * d
+
+                    @pl.when((owner >= 0) & (owner < half))
                     def _():
-                        column(owner, s, d).start()
-
-                    row(owner).start()
-                    cot_side(q).start()
+                        q = owner * 2 + b
+                        cot_arrive(q, h)
+
+                        @pl.when(reaches(d))
+                        def _():
+                            column(owner, s, d, h).start()
+
+                        row(owner, h).start()
+                        cot_side(q, h).start()
 
             from_row(a + s - 1)
 
@@ -360,7 +369,7 @@
             dev = q * 2 + core
             for d in (0, 1):
                 ring_last(dev, d).wait_recv()
-            side(xc.at[0, rows(dev)], 0, q, dev).start()
+            side(xc.at[0, rows(dev)], q, dev).start()
             early(1)
             from_row(a + half - 1)
             from_row(a - half + 1)
@@ -401,17 +410,17 @@
     for t in range(half):
         send_sum(t, 0, t == 0)
         if t == 1:
-            fill_up(n_up // 2, n_up)
+            fill_down(0, 1)
         if t + 2 < half:
             early(t + 2)
-        elif t + 2 == half:
-            pass_on(1)
         if t == 0:
             fill_up(0, n_up // 2)
-            fill_down(0, 1)
         elif t == 1:
+            fill_up(n_up // 2, n_up)
+        elif t == 2:
             fill_down(1, 2)
-    fill_down(2, n_down)
+    pass_on(1)
+    fill_down(2 if half > 2 else 1, n_down)
     pass_on(0)
     own_part.wait_recv()
     for side_of in (1, 0):
@@ -423,7 +432,8 @@
             else:
                 out_ref[:, quarters[c]] = (own[0, :, quarters[c]] + got).astype(BF16)
 
-    cot.wait_send()
+    for h in (0, 1):
+        cot_in(h).wait_send()
     own_part.wait_send()
     for d in (0, 1):
         for s in range(1, half):
@@ -434,13 +444,16 @@
 
             @pl.when(reaches(d) & (owner >= 0) & (owner < half))
             def _():
-                column(owner, s, d).wait_send()
+                for h in (0, 1):
+                    column(owner, s, d, h).wait_send()
 
     for owner in range(half):
-        row(owner).wait_send()
+        for h in (0, 1):
+            row(owner, h).wait_send()
     for r in range(n):
-        for piece in (0, 1):
-            side(xc.at[piece, rows(me)], piece, r, me).wait_send()
+        side(xc.at[0, rows(me)], r, me).wait_send()
+        for h in (0, 1):
+            cot_side(r, h).wait_send()
         remote(sibsend.at[r], sibrecv.at[r], ps_s.at[r], ps_r.at[r], here(sib)).wait_send()
 
     def told(i, _):
@@ -457,6 +470,15 @@
                     hop(d, t + 1, c).wait_send()
         for c in range(4):
             cross(d, c).wait_send()
+
+
+def put_out(*refs):
+    ins, outs, sems = refs[:3], refs[3:6], refs[6]
+    copies = [pltpu.make_async_copy(src, dst, sems.at[i]) for i, (src, dst) in enumerate(zip(ins, outs))]
+    for c in copies:
+        c.start()
+    for c in copies:
+        c.wait()
 
 
 def fused_body(ns, ep, inputs, upstream, gate_saved, expert_ids, route_weights, w_up, w_down):
@@ -503,11 +525,11 @@
             pltpu.VMEM((2, toks, width), BF16),
             dma((2 * (half + 1),)),
             dma((2 * (half + 1),)),
+            dma((4 * half,)),
             dma((2 * half,)),
-            dma((half,)),
-            dma((n,)),
             dma((2 * n,)),
-            dma((2 * n,)),
+            dma((3 * n,)),
+            dma((3 * n,)),
             dma((ep,)),
             dma((ep,)),
             dma((ep,)),
@@ -516,8 +538,8 @@
             dma((n,)),
             dma((8 * (half + 1),)),
             dma((8 * (half + 1),)),
-            dma((2,)),
-            dma((2,)),
+            dma((3,)),
+            dma((3,)),
             dma((8,)),
             dma((8,)),
             dma((3 + local,)),
@@ -529,6 +551,15 @@
         inputs[0], upstream[0], gate_saved[0].reshape(flat, ff), w_up[0],
         w_down[0].reshape(lff, width), expert_ids[0].T, route_weights[0].T,
     )
+    res = tuple(pltpu.with_memory_space_constraint(r, pltpu.VMEM) for r in (out, gup, gdn))
+    out, gup, gdn = pl.pallas_call(
+        put_out,
+        out_shape=tuple(pltpu.HBM(r.shape, r.dtype) for r in res),
+        in_specs=[vmem] * 3,
+        out_specs=(hbm, hbm, hbm),
+        scratch_shapes=[dma((3,))],
+        compiler_params=pltpu.CompilerParams(vmem_limit_bytes=2**22),
+    )(*res)
     return out[None], gup[None], gdn.reshape(1, local, ff, width)
 
 

time: 133 us -> 132 us (level)
  local copies, waits for them, and re-layouts: 3.56 us -> 0 us
  Pallas kernels: 128 us -> 131 us
    unnamed x3 -> x0, local copies, waits for them, and re-layouts: 3.56 us -> none
    pallas_call x0 -> x1, Pallas kernels: none -> 2.34 us  [fused_body(): pl.pallas_call(put_out, out_shape=tuple((pltpu.HBM(r.shape, r.dtype) for...]
where the time goes in v4:
time: 132 us
  Pallas kernels  131 us (99%)
    pallas_call x1, Pallas kernels, fused_body(): pl.pallas_call(functools.partial(kernel, ns, ep, toks, top, width, ff, lo...  129 us

profile of v4, /device:TPU:0, one launch (start us, length us, event | category | flops | bytes accessed | tf_op | source)
XLA Modules:
  0.0 131.8 jit_solution(18252101583211132430)
XLA Ops:
  0.6 128.8 %shard_map.94 = (bf16[128,1536]{1,0:T(8,128)(2,1)S(1)}, bf16[2,1536,384]{2,1,0:T(8,128)(2,1)S(1)}, bf16[768,1536]{1,0:T(8,128)(2,1)S(1)}) custom-call(bf16[128,1536]{1,0:T(8,128)(2,1)} %bitcast.17, bf16[128,1536]{1,0:T(8,128)(2,1)} %bitcast.18, bf16[1024,384]{1,0:T(8,128)(2,1)} %bitcast.16, bf16[2,1536,384]{2,1,0:T(8,128)(2,1)} %bitcast.14, ...), custom_call_target="tpu_custom_call" | custom-call | tf_op jit(solution)/shard_map/pallas_call | solution.py:495
  129.4 2.3 %shard_map.95 = (bf16[128,1536]{1,0:T(8,128)(2,1)}, bf16[2,1536,384]{2,1,0:T(8,128)(2,1)}, bf16[768,1536]{1,0:T(8,128)(2,1)}) custom-call(bf16[128,1536]{1,0:T(8,128)(2,1)S(1)} %get-tuple-element.9.refs_0_, bf16[2,1536,384]{2,1,0:T(8,128)(2,1)S(1)} %get-tuple-element.10.refs_1_, bf16[768,1536]{1,0:T(8,128)(2,1)S(1)} %get-tuple-element.11.refs_2_), custom_call_target="tpu_custom_call" | custom-call | tf_op jit(solution)/shard_map/pallas_call | solution.py:555

commit v5 on v4

--- a/solution.py
+++ b/solution.py
@@ -27,7 +27,7 @@
     ns, ep, toks, top, width, ff, local, cap,
     x_in, up_in, gate_in, wup_in, wdn_in, idt_ref, wt_ref,
     out_ref, gup_ref, gdn_ref,
-    xc, pay, paysend, idt, gate, act, slots, wflat, wup, wdn, hid, grd, part,
+    xc, pay, paysend, idt, gate, act, slots, wflat, wup, wdn, hid, grd,
     own, sibsend, sibrecv, rss, rsr, fin, finr, over,
     ring_s, ring_r, col_s, row_s, cot_r, sib_s, sib_r, pay_s, pay_r, id_s, id_r, ps_s, ps_r, rs_s, rs_r,
     y_s, y_r, over_s, over_r, loc,
@@ -250,10 +250,9 @@
             cot_side(q, h, 1 - core).wait_recv()
         g = (grd[both, :].astype(F32) * dot(xc[1, both, :], wdn[...], NT)).astype(BF16)
         grd[both, :] = g
-        part[...] = dot(g, wup[...], NT)
-        sibsend[r] = part[pl.ds(pl.multiple_of((1 - core) * toks, toks), toks), :].astype(BF16)
+        sibsend[r] = dot(grd[rows(q * 2 + 1 - core), :], wup[...], NT).astype(BF16)
         remote(sibsend.at[r], sibrecv.at[r], ps_s.at[r], ps_r.at[r], here(sib)).start()
-        own[r] = part[pl.ds(pl.multiple_of(core * toks, toks), toks), :]
+        own[r] = dot(grd[rows(q * 2 + core), :], wup[...], NT)
         return 0
 
     def hop(d, t, c):
@@ -514,7 +513,6 @@
             pltpu.VMEM((lff, width), BF16),
             pltpu.VMEM((ep * toks, lff), BF16),
             pltpu.VMEM((ep * toks, lff), BF16),
-            pltpu.VMEM((2 * toks, width), F32),
             pltpu.VMEM((n, toks, width), F32),
             pltpu.VMEM((n, toks, width), BF16),
             pltpu.VMEM((n, toks, width), BF16),

time: 132 us -> 133 us (level)
  no operation moved by 1% of the time
where the time goes in v5:
time: 133 us
  Pallas kernels  132 us (99%)
    pallas_call x1, Pallas kernels, fused_body(): pl.pallas_call(functools.partial(kernel, ns, ep, toks, top, width, ff, lo...  130 us

profile of v5, /device:TPU:0, one launch (start us, length us, event | category | flops | bytes accessed | tf_op | source)
XLA Modules:
  0.0 133.0 jit_solution(5382431836119373455)
XLA Ops:
  0.6 130.0 %shard_map.94 = (bf16[128,1536]{1,0:T(8,128)(2,1)S(1)}, bf16[2,1536,384]{2,1,0:T(8,128)(2,1)S(1)}, bf16[768,1536]{1,0:T(8,128)(2,1)S(1)}) custom-call(bf16[128,1536]{1,0:T(8,128)(2,1)} %bitcast.17, bf16[128,1536]{1,0:T(8,128)(2,1)} %bitcast.18, bf16[1024,384]{1,0:T(8,128)(2,1)} %bitcast.16, bf16[2,1536,384]{2,1,0:T(8,128)(2,1)} %bitcast.14, ...), custom_call_target="tpu_custom_call" | custom-call | tf_op jit(solution)/shard_map/pallas_call | solution.py:494
  130.6 2.3 %shard_map.95 = (bf16[128,1536]{1,0:T(8,128)(2,1)}, bf16[2,1536,384]{2,1,0:T(8,128)(2,1)}, bf16[768,1536]{1,0:T(8,128)(2,1)}) custom-call(bf16[128,1536]{1,0:T(8,128)(2,1)S(1)} %get-tuple-element.9.refs_0_, bf16[2,1536,384]{2,1,0:T(8,128)(2,1)S(1)} %get-tuple-element.10.refs_1_, bf16[768,1536]{1,0:T(8,128)(2,1)S(1)} %get-tuple-element.11.refs_2_), custom_call_target="tpu_custom_call" | custom-call | tf_op jit(solution)/shard_map/pallas_call | solution.py:553
